TPU v7x, 256 devices: a whole 4x4x8 slice. The times are simulated.
256 devices in a mesh: seq: 16 (over y, z_hi, core), tp: 16 (over x, z_lo).
Axes of the slice: x: 4, y: 4, z: 8 (z_hi: 2, z_lo: 4; z = z_hi * 4 + z_lo), core: 2. Of those that a mesh axis runs over, the one named last changes fastest.
Arguments:
- tokens: bfloat16 [8192, 4608], P(('seq', 'tp')), may hold values from -6 to 6
- norm_gain: float32 [4608], replicated, may hold values from 0.1 to 1.9
- query_weight: bfloat16 [4608, 4096], P(None, 'tp'), may hold values from -6 to 6
- key_matrix: bfloat16 [4608, 2048], P(None, 'tp'), may hold values from -0.09375 to 0.09375
- value_matrix: bfloat16 [4608, 2048], P(None, 'tp'), may hold values from -0.09375 to 0.09375
- output_grad: bfloat16 [8192, 4096], P('seq', 'tp'), may hold values from -3 to 3
Outputs:
- input_gradient: bfloat16 [8192, 4608], P(('seq', 'tp'))
All inputs are finite; a program needn't handle non-finite values.
Results may differ from a plain program's by a relative error of at most 0.014.
The roundings to bfloat16 on the way count: a program that leaves them out, or rounds other values in their place, can miss the bound.
Values may be sent and summed in bfloat16 or wider, within the bound.
A program may use at most 64 MiB of HBM per device.

v0:
```python
import jax
import jax.numpy as jnp
from jax import lax
from jax.sharding import Mesh
from jax.sharding import PartitionSpec as P

HEAD_SIZE = 128
WINDOW = 640
TP = ("tp_0", "tp_1")
SEQ_TP = ("seq", "tp_0", "tp_1")


SCALE = 1.0 / 12.0
CAP = 50.0
EPS = 1e-06


def shifted(block, axis, distance):
    devices = range(lax.axis_size(axis))
    route = [(i - distance, i) for i in devices if i - distance in devices]
    return lax.ppermute(block, axis, route)


def sum_by_axis(terms, axes):
    so_far = terms.astype(jnp.bfloat16)
    for axis in axes:
        so_far = lax.psum_scatter(so_far, axis, scatter_dimension=0, tiled=True)
    return so_far.astype(jnp.float32)


def normalize_project(rows_piece, norm_gain, query_weight, key_matrix, value_matrix):
    float_values = rows_piece.astype(jnp.float32)
    reciprocal_norm = lax.rsqrt(jnp.mean(float_values * float_values, axis=1, keepdims=True) + EPS)
    normed = (float_values * reciprocal_norm * norm_gain).astype(jnp.bfloat16)
    outputs = [
        jnp.dot(normed, weight, preferred_element_type=jnp.float32).astype(jnp.bfloat16)
        for weight in (query_weight, key_matrix, value_matrix)
    ]
    return jnp.concatenate(outputs, axis=1)


def block_grads(query_blk, grad_blk, key_blk, value_blk, query_pos, key_pos):
    row_count = query_blk.shape[0]
    key_span = key_blk.shape[0]
    kv_heads = key_blk.shape[1] // HEAD_SIZE
    groups = query_blk.shape[1] // key_blk.shape[1]
    query_four = query_blk.reshape(row_count, kv_heads, groups, HEAD_SIZE)
    grad_four = grad_blk.reshape(row_count, kv_heads, groups, HEAD_SIZE)
    key_three = key_blk.reshape(key_span, kv_heads, HEAD_SIZE)
    value_three = value_blk.reshape(key_span, kv_heads, HEAD_SIZE)
    raw = jnp.einsum("qkgd,skd->kgqs", query_four, key_three, preferred_element_type=jnp.float32)
    bent = jnp.tanh(raw * SCALE / CAP)
    capped = CAP * bent
    valid = (
        (key_pos[None, :] <= query_pos[:, None])
        & (key_pos[None, :] > query_pos[:, None] - WINDOW)
        & (key_pos[None, :] >= 0)
    )
    expo = jnp.where(valid, jnp.exp(capped), 0.0)
    probs = expo / jnp.sum(expo, axis=-1, keepdims=True)
    d_probs = jnp.einsum(
        "qkgd,skd->kgqs", grad_four, value_three, preferred_element_type=jnp.float32
    )
    delta = jnp.sum(probs * d_probs, axis=-1, keepdims=True)
    d_raw = (probs * (d_probs - delta) * (1.0 - bent * bent) * SCALE).astype(jnp.bfloat16)
    probs_low = probs.astype(jnp.bfloat16)
    grad_query = jnp.einsum(
        "kgqs,skd->qkgd", d_raw, key_three, preferred_element_type=jnp.float32
    ).reshape(row_count, kv_heads * groups * HEAD_SIZE)
    grad_key = jnp.einsum(
        "kgqs,qkgd->skd", d_raw, query_four, preferred_element_type=jnp.float32
    ).reshape(key_span, kv_heads * HEAD_SIZE)
    grad_value = jnp.einsum(
        "kgqs,qkgd->skd", probs_low, grad_four, preferred_element_type=jnp.float32
    ).reshape(key_span, kv_heads * HEAD_SIZE)
    return (grad_query, grad_key, grad_value)


def row_product(grad_rows, weight):
    return lax.dot_general(
        grad_rows, weight, (((1,), (1,)), ((), ())), preferred_element_type=jnp.float32
    )


def on_device(tokens, norm_gain, query_weight, key_matrix, value_matrix, output_grad):
    local_rows = output_grad.shape[0]
    query_cols = query_weight.shape[1]
    key_cols = key_matrix.shape[1]
    reach = WINDOW - local_rows
    block_rows = min(512, local_rows)
    key_span = WINDOW + block_rows
    joined = normalize_project(
        lax.all_gather(tokens, TP, axis=0, tiled=True),
        norm_gain,
        query_weight,
        key_matrix,
        value_matrix,
    )
    query_own = joined[:, :query_cols]
    key_own = joined[:, query_cols : query_cols + key_cols]
    value_own = joined[:, query_cols + key_cols :]
    near_key, near_value = shifted((key_own, value_own), "seq", 1)
    far_key, far_value = shifted(
        (key_own[local_rows - reach :], value_own[local_rows - reach :]), "seq", 2
    )
    all_key = jnp.concatenate([far_key, near_key, key_own], axis=0)
    all_value = jnp.concatenate([far_value, near_value, value_own], axis=0)
    anchor = lax.axis_index("seq") * local_rows
    acc_key = jnp.zeros((WINDOW + local_rows, key_cols), jnp.float32)
    acc_value = jnp.zeros((WINDOW + local_rows, key_cols), jnp.float32)
    query_pos = anchor + 0 + jnp.arange(block_rows, dtype=jnp.int32)
    key_pos = anchor + 0 - WINDOW + jnp.arange(key_span, dtype=jnp.int32)
    grad_query, grad_key, grad_value = block_grads(
        query_own, output_grad, all_key, all_value, query_pos, key_pos
    )
    acc_key = acc_key.at[0:key_span].add(grad_key)
    acc_value = acc_value.at[0:key_span].add(grad_value)
    query_grads = grad_query.astype(jnp.bfloat16)
    far_gkey = acc_key[:reach]
    far_gvalue = acc_value[:reach]
    near_gkey = acc_key[reach : reach + local_rows]
    near_gvalue = acc_value[reach : reach + local_rows]
    own_gkey = acc_key[reach + local_rows :]
    own_gvalue = acc_value[reach + local_rows :]
    far_back_key, far_back_value = shifted((far_gkey, far_gvalue), "seq", -2)
    back_key, back_value = shifted((near_gkey, near_gvalue), "seq", -1)
    own_gkey = own_gkey + back_key
    own_gvalue = own_gvalue + back_value
    own_gkey = own_gkey.at[local_rows - reach :].add(far_back_key)
    own_gvalue = own_gvalue.at[local_rows - reach :].add(far_back_value)
    key_low = own_gkey.astype(jnp.bfloat16)
    value_low = own_gvalue.astype(jnp.bfloat16)
    total_term = row_product(query_grads, query_weight)
    total_term = total_term + row_product(key_low, key_matrix)
    d_norm = sum_by_axis(total_term + row_product(value_low, value_matrix), TP)
    float_values = tokens.astype(jnp.float32)
    reciprocal_norm = lax.rsqrt(jnp.mean(float_values * float_values, axis=1, keepdims=True) + EPS)
    upper_limit = d_norm * norm_gain
    normalized_input = float_values * reciprocal_norm
    input_gradient = reciprocal_norm * (
        upper_limit
        - normalized_input * jnp.mean(upper_limit * normalized_input, axis=1, keepdims=True)
    )
    return input_gradient.astype(jnp.bfloat16)


def solution(mesh):
    finer = Mesh(mesh.devices.reshape(mesh.shape["seq"], 4, 4), ("seq", "tp_0", "tp_1"))
    in_specs = (P(SEQ_TP, None), P(), P(None, TP), P(None, TP), P(None, TP), P("seq", TP))
    out_specs = P(SEQ_TP, None)
    return jax.shard_map(
        on_device, mesh=finer, in_specs=in_specs, out_specs=out_specs, check_vma=False
    )
```

profile of v0, /device:TPU:24, one launch (start us, length us, event | category | flops | bytes accessed | tf_op | source)
XLA Modules:
  0.0 295.9 jit_solution(13565475252285906902)
XLA Ops:
  6.5 0.0 copy-start
  6.5 0.0 copy-start.5
  6.5 0.0 all-gather.2.cloned.1.call-start
  6.5 0.7 all-gather.2.cloned.1.call-update
  7.3 0.0 reduce-scatter.3.cloned.1.call-start
  7.4 0.9 and_and_fusion
  8.3 116.0 %all-gather.2.cloned.1.call-done = bf16[512,4608]{1,0:T(8,128)(2,1)} async-done(((bf16[32,4608]{1,0:T(8,128)(2,1)}), bf16[512,4608]{1,0:T(8,128)(2,1)}) %all-gather.2.cloned.1.call-update) | async-done | bytes 4718608 | tf_op jit(solution)/shard_map/all_gather | solution.py:93
  124.3 0.0 copy-start.1
  124.3 3.5 %fusion = f32[512]{0:T(512)S(1)} fusion(bf16[512,4608]{1,0:T(8,128)(2,1)} %all-gather.2.cloned.1.call-done), kind=kLoop, calls=%fused_computation.2 | loop fusion | flops 7077376 | bytes 4720640 | tf_op jit(solution)/shard_map/reduce_sum | solution.py:33
  127.8 0.0 copy-done.5
  127.8 0.3 copy-done.1
  128.1 0.0 copy-start.3
  128.1 2.8 convolution_convert_fusion.3
  130.9 1.9 collective-permute-start.1
  132.8 0.0 copy-done.3
  132.8 1.4 convolution_convert_fusion.2
  134.3 5.1 %collective-permute-start.3 = (bf16[512,128]{1,0:T(8,128)(2,1)S(1)}, bf16[512,128]{1,0:T(8,128)(2,1)S(1)}, u32[]{:S(2)}, u32[]{:S(2)}) collective-permute-start(bf16[512,128]{1,0:T(8,128)(2,1)S(1)} %convolution_convert_fusion.2), channel_id=1, source_target_pairs={{0,16},{16,32},{32,48},{48,64},{64,80},{80,96},{96,112},{112,128},... | collective-permute-start | bytes 393224 | tf_op jit(solution)/shard_map/ppermute | solution.py:21
  139.4 1.9 collective-permute-start
  141.3 2.1 collective-permute-start.2
  143.4 0.0 copy-done
  143.4 1.8 convolution_convert_fusion.1
  145.2 4.8 %collective-permute-done = bf16[128,128]{1,0:T(8,128)(2,1)S(1)} collective-permute-done((bf16[128,128]{1,0:T(8,128)(2,1)S(1)}, bf16[128,128]{1,0:T(8,128)(2,1)S(1)}, u32[]{:S(2)}, u32[]{:S(2)}) %collective-permute-start) | collective-permute-done | bytes 32800 | tf_op jit(solution)/shard_map/ppermute | solution.py:21
  150.0 0.0 collective-permute-done.1
  150.0 0.0 copy-start.6
  150.0 1.7 fusion.8
  151.7 0.0 copy-done.6
  151.7 1.4 fusion.10
  153.2 0.0 collective-permute-done.2
  153.2 0.0 collective-permute-done.3
  153.2 1.8 fusion.5
  155.1 2.2 fusion.9
  157.3 0.9 convolution_bitcast_fusion
  158.2 4.7 %collective-permute-start.6 = (f32[512,128]{1,0:T(8,128)S(1)}, f32[512,128]{1,0:T(8,128)S(1)}, u32[]{:S(2)}, u32[]{:S(2)}) collective-permute-start(f32[512,128]{1,0:T(8,128)S(1)} %slice.123), channel_id=1, source_target_pairs={{16,0},{32,16},{48,32},{64,48},{80,64},{96,80},{112,96},{128,112},... | collective-permute-start | bytes 786440 | tf_op jit(solution)/shard_map/ppermute | solution.py:21
  162.9 6.2 %collective-permute-start.7 = (f32[128,128]{1,0:T(8,128)S(1)}, f32[128,128]{1,0:T(8,128)S(1)}, u32[]{:S(2)}, u32[]{:S(2)}) collective-permute-start(f32[128,128]{1,0:T(8,128)S(1)} %slice.125), channel_id=1, source_target_pairs={{32,0},{48,16},{64,32},{80,48},{96,64},{112,80},{128,96},{144,112}... | collective-permute-start | bytes 196616 | tf_op jit(solution)/shard_map/ppermute | solution.py:21
  169.1 3.1 %collective-permute-start.4 = (f32[512,128]{0,1:T(8,128)S(1)}, f32[512,128]{0,1:T(8,128)S(1)}, u32[]{:S(2)}, u32[]{:S(2)}) collective-permute-start(f32[512,128]{0,1:T(8,128)S(1)} %slice_bitcast_fusion.1), channel_id=1, source_target_pairs={{16,0},{32,16},{48,32},{64,48},{80,64},{96,80},{112,96},{128,112},... | collective-permute-start | bytes 786440 | tf_op jit(solution)/shard_map/ppermute | solution.py:21
  172.2 5.5 %collective-permute-start.5 = (f32[128,128]{0,1:T(8,128)S(1)}, f32[128,128]{0,1:T(8,128)S(1)}, u32[]{:S(2)}, u32[]{:S(2)}) collective-permute-start(f32[128,128]{0,1:T(8,128)S(1)} %slice_bitcast_fusion.3), channel_id=1, source_target_pairs={{32,0},{48,16},{64,32},{80,48},{96,64},{112,80},{128,96},{144,112}... | collective-permute-start | bytes 196616 | tf_op jit(solution)/shard_map/ppermute | solution.py:21
  177.7 0.5 convolution_convert_fusion
  178.3 0.0 copy-start.4
  178.3 1.4 fusion.45
  179.7 0.9 collective-permute-done.4
  180.6 3.5 %collective-permute-done.5 = f32[128,128]{0,1:T(8,128)S(1)} collective-permute-done((f32[128,128]{0,1:T(8,128)S(1)}, f32[128,128]{0,1:T(8,128)S(1)}, u32[]{:S(2)}, u32[]{:S(2)}) %collective-permute-start.5) | collective-permute-done | bytes 65568 | tf_op jit(solution)/shard_map/ppermute | solution.py:21
  184.2 0.0 copy-done.4
  184.2 5.1 %fusion.33 = f32[512,4608]{1,0:T(8,128)} fusion(bf16[4608,128]{1,0:T(8,128)(2,1)S(1)} %copy-done.4, f32[512,128]{0,1:T(8,128)S(1)} %fusion.36), kind=kOutput, calls=%fused_computation.54 | convolution fusion | flops 604045312 | bytes 10878976 | tf_op jit(solution)/shard_map/dot_general | solution.py:80
  189.2 0.0 collective-permute-done.6
  189.3 0.0 collective-permute-done.7
  189.3 7.7 %add_convert_fusion = bf16[512,4608]{1,0:T(8,128)(2,1)} fusion(f32[512,4608]{1,0:T(8,128)S(1)} %fusion.45, f32[512,4608]{1,0:T(8,128)} %fusion.33, bf16[4608,128]{1,0:T(8,128)(2,1)S(1)} %copy-done.3, f32[512,128]{1,0:T(8,128)S(1)} %fusion.35), kind=kOutput, calls=%fused_computation.5 | convolution fusion | flops 611123200 | bytes 25034752 | tf_op jit(solution)/shard_map/dot_general | solution.py:80
  197.0 0.0 copy-start.2
  197.0 0.0 reduce-scatter.3.cloned.1.call-update
  197.0 0.0 reduce-scatter.5.cloned.1.call-start
  197.1 52.2 %reduce-scatter.3.cloned.1.call-done = bf16[128,4608]{1,0:T(8,128)(2,1)} async-done(((bf16[512,4608]{1,0:T(8,128)(2,1)}), bf16[128,4608]{1,0:T(8,128)(2,1)}) %reduce-scatter.3.cloned.1.call-update) | async-done | bytes 1179664 | tf_op jit(solution)/shard_map/reduce_scatter | solution.py:27
  249.3 0.0 reduce-scatter.5.cloned.1.call-update
  249.3 0.0 copy-done.2
  249.3 0.2 fusion.20
  249.5 36.8 %reduce-scatter.5.cloned.1.call-done = bf16[32,4608]{1,0:T(8,128)(2,1)} async-done(((bf16[128,4608]{1,0:T(8,128)(2,1)}), bf16[32,4608]{1,0:T(8,128)(2,1)}) %reduce-scatter.5.cloned.1.call-update) | async-done | bytes 294928 | tf_op jit(solution)/shard_map/reduce_scatter | solution.py:27
  286.3 1.2 fusion.16
  287.5 1.9 fusion.19
  (16 shorter events, 0.2 us)
Async XLA Ops:
  6.5 136.9 %copy-start = (bf16[4608,256]{1,0:T(8,128)(2,1)S(1)}, bf16[4608,256]{1,0:T(8,128)(2,1)}, u32[]{:S(2)}) copy-start(bf16[4608,256]{1,0:T(8,128)(2,1)} %param.20) | copy-start | bytes 7077892
  6.5 121.3 %copy-start.5 = (f32[4608]{0:T(1024)S(1)}, f32[4608]{0:T(1024)}, u32[]{:S(2)}) copy-start(f32[4608]{0:T(1024)} %param.19) | copy-start | bytes 55300
  6.5 117.8 %all-gather.2.cloned.1.call-start = ((), (), s32[]{:S(2)}) async-start(), calls=%async_computation.2 | async-start | bytes 5013504 | tf_op jit(solution)/shard_map/all_gather | solution.py:93
  7.3 242.0 %reduce-scatter.3.cloned.1.call-start = ((), (), s32[]{:S(2)}) async-start(), calls=%async_computation.3 | async-start | bytes 5898240 | tf_op jit(solution)/shard_map/reduce_scatter | solution.py:27
  124.3 3.8 %copy-start.1 = (bf16[512,4608]{1,0:T(8,128)(2,1)S(1)}, bf16[512,4608]{1,0:T(8,128)(2,1)}, u32[]{:S(2)}) copy-start(bf16[512,4608]{1,0:T(8,128)(2,1)} %all-gather.2.cloned.1.call-done) | copy-start | bytes 14155780
  128.1 4.8 %copy-start.3 = (bf16[4608,128]{1,0:T(8,128)(2,1)S(1)}, bf16[4608,128]{1,0:T(8,128)(2,1)}, u32[]{:S(2)}) copy-start(bf16[4608,128]{1,0:T(8,128)(2,1)} %param.22) | copy-start | bytes 3538948
  130.9 19.1 %collective-permute-start.1 = (bf16[512,128]{1,0:T(8,128)(2,1)S(1)}, bf16[512,128]{1,0:T(8,128)(2,1)S(1)}, u32[]{:S(2)}, u32[]{:S(2)}) collective-permute-start(bf16[512,128]{1,0:T(8,128)(2,1)S(1)} %convolution_convert_fusion.3), channel_id=1, source_target_pairs={{0,16},{16,32},{32,48},{48,64},{64,80},{80,96},{96,112},{112,128},... | collective-permute-start | bytes 393224 | tf_op jit(solution)/shard_map/ppermute | solution.py:21
  134.3 18.9 %collective-permute-start.3 = (bf16[512,128]{1,0:T(8,128)(2,1)S(1)}, bf16[512,128]{1,0:T(8,128)(2,1)S(1)}, u32[]{:S(2)}, u32[]{:S(2)}) collective-permute-start(bf16[512,128]{1,0:T(8,128)(2,1)S(1)} %convolution_convert_fusion.2), channel_id=1, source_target_pairs={{0,16},{16,32},{32,48},{48,64},{64,80},{80,96},{96,112},{112,128},... | collective-permute-start | bytes 393224 | tf_op jit(solution)/shard_map/ppermute | solution.py:21
  139.4 10.6 %collective-permute-start = (bf16[128,128]{1,0:T(8,128)(2,1)S(1)}, bf16[128,128]{1,0:T(8,128)(2,1)S(1)}, u32[]{:S(2)}, u32[]{:S(2)}) collective-permute-start(bf16[128,128]{1,0:T(8,128)(2,1)S(1)} %slice.116), channel_id=1, source_target_pairs={{0,32},{16,48},{32,64},{48,80},{64,96},{80,112},{96,128},{112,144}... | collective-permute-start | bytes 98312 | tf_op jit(solution)/shard_map/ppermute | solution.py:21
  141.3 11.9 %collective-permute-start.2 = (bf16[128,128]{1,0:T(8,128)(2,1)S(1)}, bf16[128,128]{1,0:T(8,128)(2,1)S(1)}, u32[]{:S(2)}, u32[]{:S(2)}) collective-permute-start(bf16[128,128]{1,0:T(8,128)(2,1)S(1)} %slice.117), channel_id=1, source_target_pairs={{0,32},{16,48},{32,64},{48,80},{64,96},{80,112},{96,128},{112,144}... | collective-permute-start | bytes 98312 | tf_op jit(solution)/shard_map/ppermute | solution.py:21
  150.0 1.7 copy-start.6
  158.2 31.0 %collective-permute-start.6 = (f32[512,128]{1,0:T(8,128)S(1)}, f32[512,128]{1,0:T(8,128)S(1)}, u32[]{:S(2)}, u32[]{:S(2)}) collective-permute-start(f32[512,128]{1,0:T(8,128)S(1)} %slice.123), channel_id=1, source_target_pairs={{16,0},{32,16},{48,32},{64,48},{80,64},{96,80},{112,96},{128,112},... | collective-permute-start | bytes 786440 | tf_op jit(solution)/shard_map/ppermute | solution.py:21
  162.9 26.3 %collective-permute-start.7 = (f32[128,128]{1,0:T(8,128)S(1)}, f32[128,128]{1,0:T(8,128)S(1)}, u32[]{:S(2)}, u32[]{:S(2)}) collective-permute-start(f32[128,128]{1,0:T(8,128)S(1)} %slice.125), channel_id=1, source_target_pairs={{32,0},{48,16},{64,32},{80,48},{96,64},{112,80},{128,96},{144,112}... | collective-permute-start | bytes 196616 | tf_op jit(solution)/shard_map/ppermute | solution.py:21
  169.1 11.5 %collective-permute-start.4 = (f32[512,128]{0,1:T(8,128)S(1)}, f32[512,128]{0,1:T(8,128)S(1)}, u32[]{:S(2)}, u32[]{:S(2)}) collective-permute-start(f32[512,128]{0,1:T(8,128)S(1)} %slice_bitcast_fusion.1), channel_id=1, source_target_pairs={{16,0},{32,16},{48,32},{64,48},{80,64},{96,80},{112,96},{128,112},... | collective-permute-start | bytes 786440 | tf_op jit(solution)/shard_map/ppermute | solution.py:21
  172.2 12.0 %collective-permute-start.5 = (f32[128,128]{0,1:T(8,128)S(1)}, f32[128,128]{0,1:T(8,128)S(1)}, u32[]{:S(2)}, u32[]{:S(2)}) collective-permute-start(f32[128,128]{0,1:T(8,128)S(1)} %slice_bitcast_fusion.3), channel_id=1, source_target_pairs={{32,0},{48,16},{64,32},{80,48},{96,64},{112,80},{128,96},{144,112}... | collective-permute-start | bytes 196616 | tf_op jit(solution)/shard_map/ppermute | solution.py:21
  178.3 5.9 %copy-start.4 = (bf16[4608,128]{1,0:T(8,128)(2,1)S(1)}, bf16[4608,128]{1,0:T(8,128)(2,1)}, u32[]{:S(2)}) copy-start(bf16[4608,128]{1,0:T(8,128)(2,1)} %param.21) | copy-start | bytes 3538948
  197.0 52.3 %copy-start.2 = (bf16[32,4608]{1,0:T(8,128)(2,1)S(1)}, bf16[32,4608]{1,0:T(8,128)(2,1)}, u32[]{:S(2)}) copy-start(bf16[32,4608]{1,0:T(8,128)(2,1)} %param.18) | copy-start | bytes 884740
  197.0 89.3 %reduce-scatter.5.cloned.1.call-start = ((), (), s32[]{:S(2)}) async-start(), calls=%async_computation.4 | async-start | bytes 1474560 | tf_op jit(solution)/shard_map/reduce_scatter | solution.py:27
Sparse Core Ops, SparseCore 0:
  9.1 115.1 all-gather.1
  197.2 52.0 reduce-scatter.2
  251.9 34.3 reduce-scatter.4
where the time goes:
time: 297 us; the launch traced here: 296 us
  waiting for transfers between devices  215 us (72%)
  starting transfers between devices  30.6 us (10%)
  matrix products  26.6 us (9%)
  between operations  13.4 us (5%)
  other arithmetic  10 us (3%)
    all_gather x1, waiting for transfers between devices, on_device(): lax.all_gather(tokens, TP, axis=0, tiled=True)  116 us
    reduce_scatter x2, waiting for transfers between devices, sum_by_axis(): so_far = lax.psum_scatter(so_far, axis, scatter_dimension=0, tiled=True)  89 us
    ppermute x8, starting transfers between devices, shifted(): return lax.ppermute(block, axis, route)  30.5 us
    dot_general x3, matrix products, row_product(): lax.dot_general(grad_rows, weight, (((1,), (1,)), ((), ())), preferred_el...  14.2 us
    ppermute x8, waiting for transfers between devices, shifted(): return lax.ppermute(block, axis, route)  9.16 us
    dot_general x3, matrix products, normalize_project(): jnp.dot(normed, weight, preferred_element_type=jnp.float32)  6.05 us
  transfers between devices with their start and end apart: 11, of which 6 were waited for; matrix products, arithmetic and copies ran while one was open for 5% of the time, Pallas kernels for 0%

commit v1 on v0

v1 whole, which is shorter than its diff:
```python
import functools

import jax
import jax.numpy as jnp
from jax import lax
from jax.experimental import pallas as pl
from jax.experimental.pallas import tpu as pltpu
from jax.sharding import PartitionSpec as P

HEAD_SIZE = 128
WINDOW = 640
SCALE = 1.0 / 12.0
CAP = 50.0
EPS = 1e-06
MESH = pl.DeviceIdType.MESH
NX = 4
NZ = 4
A_TILES = 8


def place():
    t = lax.axis_index("tp")
    return t // NZ, t % NZ


def near_to_far(z):
    def high(q):
        return (q, 5 - q, jnp.int32(1), jnp.int32(0))

    up = high(z)
    low = high(3 - z)
    return [jnp.where(z >= 2, u, 3 - v) for u, v in zip(up, low)]


def send_to(src, dst, send_sem, recv_sem, tp):
    return pltpu.make_async_remote_copy(
        src_ref=src,
        dst_ref=dst,
        send_sem=send_sem,
        recv_sem=recv_sem,
        device_id={"tp": tp},
        device_id_type=MESH,
    )


def tp_of(x, z):
    return x * NZ + z


def greet_plane(x, z):
    barrier = pltpu.get_barrier_semaphore()

    def greet(tp):
        pl.semaphore_signal(barrier, inc=1, device_id={"tp": tp}, device_id_type=MESH)

    greet(tp_of((x + 1) % NX, z))
    greet(tp_of((x + 3) % NX, z))

    @pl.when(z > 0)
    def _():
        greet(tp_of(x, z - 1))

    @pl.when(z < NZ - 1)
    def _():
        greet(tp_of(x, z + 1))

    return barrier


def await_plane(barrier, z):
    edge = (z == 0) | (z == NZ - 1)
    pl.semaphore_wait(barrier, jnp.where(edge, 3, 4))


class Sends:
    def __init__(self):
        self.started = []

    def start(self, copy, when=None):
        self.started.append((copy, when))
        if when is None:
            copy.start()
        else:
            pl.when(when)(lambda: copy.start())

    def finish(self):
        for copy, when in self.started:
            if when is None:
                copy.wait_send()
            else:
                pl.when(when)(lambda copy=copy: copy.wait_send())


def gather_project(
    tokens_ref, gain_ref, wq_ref, wk_ref, wv_ref, out_ref,
    g, w, w_sem, sx, rx, szb, rzb, sza, rza,
):
    x, z = place()
    rows, width = tokens_ref.shape
    half = rows // 2
    a_cols = pl.ds(0, A_TILES * 128)
    b_cols = pl.ds(A_TILES * 128, width - A_TILES * 128)
    xp, xm, xo = (x + 1) % NX, (x + 3) % NX, (x + 2) % NX
    zs = near_to_far(z)
    q_cols, k_cols = wq_ref.shape[1], wk_ref.shape[1]
    barrier = greet_plane(x, z)
    loads = [
        pltpu.make_async_copy(wq_ref, w.at[:, pl.ds(0, q_cols)], w_sem.at[0]),
        pltpu.make_async_copy(wk_ref, w.at[:, pl.ds(q_cols, k_cols)], w_sem.at[1]),
        pltpu.make_async_copy(wv_ref, w.at[:, pl.ds(q_cols + k_cols, k_cols)], w_sem.at[2]),
    ]
    for load in loads:
        load.start()
    values = tokens_ref[...].astype(jnp.float32)
    inv = lax.rsqrt(jnp.mean(values * values, axis=1, keepdims=True) + EPS)
    g[z, pl.ds(x * rows, rows), :] = (values * inv * gain_ref[...]).astype(jnp.bfloat16)
    await_plane(barrier, z)
    sends = Sends()

    def part(zr, xr, h, cols):
        if h is None:
            return g.at[zr, pl.ds(pl.multiple_of(xr * rows, rows), rows), cols]
        return g.at[zr, pl.ds(pl.multiple_of(xr * rows + h * half, half), half), cols]

    def x_send(k, zr, xr, h, cols, to, direction, slot, when=None):
        piece = part(zr, xr, h, cols)
        p = 1 if k == NZ else 0
        sends.start(
            send_to(piece, piece, sx.at[direction, k, slot], rx.at[p, zr, xr, h], tp_of(to, z)), when
        )

    def x_wait(k, zr, xr, h, cols):
        piece = part(zr, xr, h, cols)
        p = 1 if k == NZ else 0
        send_to(piece, piece, sx.at[0, k, 0], rx.at[p, zr, xr, h], tp_of(xp, z)).wait_recv()

    def x_own(k, zr, cols, first):
        h_right, h_left = (0, 1) if first else (1, 0)
        slot = 0 if first else 1
        x_send(k, zr, x, h_right, cols, xp, 0, slot)
        x_send(k, zr, x, h_left, cols, xm, 1, slot)

    def x_forward(k, zr, cols):
        x_wait(k, zr, xm, 0, cols)
        x_send(k, zr, xm, 0, cols, xp, 0, 2)
        x_wait(k, zr, xp, 1, cols)
        x_send(k, zr, xp, 1, cols, xm, 1, 2)

    def x_rest(k, zr, cols):
        x_wait(k, zr, xm, 1, cols)
        x_wait(k, zr, xp, 0, cols)
        x_wait(k, zr, xo, 0, cols)
        x_wait(k, zr, xo, 1, cols)

    def z_piece(zr, is_a):
        return g.at[zr, :, a_cols] if is_a else part(zr, x, None, b_cols)

    def z_send(k, zr, is_a):
        piece = z_piece(zr, is_a)
        ss, rs = (sza, rza) if is_a else (szb, rzb)
        up = send_to(piece, piece, ss.at[0, k], rs.at[zr], tp_of(x, jnp.minimum(z + 1, NZ - 1)))
        down = send_to(piece, piece, ss.at[1, k], rs.at[zr], tp_of(x, jnp.maximum(z - 1, 0)))
        sends.start(up, (zr <= z) & (z < NZ - 1))
        sends.start(down, (zr >= z) & (z > 0))

    def z_wait(zr, is_a):
        piece = z_piece(zr, is_a)
        ss, rs = (sza, rza) if is_a else (szb, rzb)
        send_to(piece, piece, ss.at[0, 0], rs.at[zr], tp_of(xp, z)).wait_recv()

    def project(zr):
        for load in loads if not project.loaded else []:
            load.wait()
        project.loaded = True
        out = jnp.dot(g[zr], w[...], preferred_element_type=jnp.float32).astype(jnp.bfloat16)
        for i in range(NX):
            at = pl.multiple_of(i * NZ * rows + zr * rows, rows)
            out_ref[pl.ds(at, rows), :] = out[i * rows : (i + 1) * rows]

    project.loaded = False

    x_own(NZ, z, a_cols, True)
    x_own(NZ, z, a_cols, False)
    z_send(0, z, False)
    x_own(0, z, b_cols, True)
    x_forward(NZ, z, a_cols)
    x_own(0, z, b_cols, False)
    x_rest(NZ, z, a_cols)
    z_send(0, z, True)
    for k in range(1, NZ):
        zr, before = zs[k], zs[k - 1]
        x_forward(k - 1, before, b_cols)
        z_wait(zr, False)
        z_send(k, zr, False)
        x_own(k, zr, b_cols, True)
        x_own(k, zr, b_cols, False)
        z_wait(zr, True)
        z_send(k, zr, True)
        x_rest(k - 1, before, b_cols)
        project(before)
    x_forward(NZ - 1, zs[-1], b_cols)
    x_rest(NZ - 1, zs[-1], b_cols)
    project(zs[-1])
    sends.finish()


def gather_project_call(tokens, gain, wq, wk, wv):
    rows, width = tokens.shape
    cols = wq.shape[1] + 2 * wk.shape[1]
    vmem = pl.BlockSpec(memory_space=pltpu.VMEM)
    any_space = pl.BlockSpec(memory_space=pl.ANY)
    dma = pltpu.SemaphoreType.DMA
    return pl.pallas_call(
        gather_project,
        out_shape=jax.ShapeDtypeStruct((rows * NX * NZ, cols), jnp.bfloat16),
        in_specs=[vmem, vmem, any_space, any_space, any_space],
        out_specs=vmem,
        scratch_shapes=[
            pltpu.VMEM((NZ, NX * rows, width), jnp.bfloat16),
            pltpu.VMEM((width, cols), jnp.bfloat16),
            dma((3,)),
            dma((2, NZ + 1, 3)),
            dma((2, NZ, NX, 2)),
            dma((2, NZ)),
            dma((NZ,)),
            dma((2, NZ)),
            dma((NZ,)),
        ],
        compiler_params=pltpu.CompilerParams(
            collective_id=0, has_side_effects=True, vmem_limit_bytes=40 * 1024 * 1024
        ),
    )(tokens, gain, wq, wk, wv)


def product_scatter(
    tokens_ref, gain_ref, grads_ref, wq_ref, wk_ref, wv_ref, out_ref,
    p, w, total, got_opp, got_x, got_za, got_zb, w_sem, s1, r1, s2, r2, sza, rza, szb, rzb,
):
    x, z = place()
    rows, width = tokens_ref.shape
    half = rows // 2
    a_width = A_TILES * 128
    a_cols = pl.ds(0, a_width)
    b_cols = pl.ds(a_width, width - a_width)
    xp, xm, xo = (x + 1) % NX, (x + 3) % NX, (x + 2) % NX
    zs = near_to_far(z)[::-1]
    q_cols, k_cols = wq_ref.shape[1], wk_ref.shape[1]
    barrier = greet_plane(x, z)
    loads = [
        pltpu.make_async_copy(wq_ref, w.at[:, pl.ds(0, q_cols)], w_sem.at[0]),
        pltpu.make_async_copy(wk_ref, w.at[:, pl.ds(q_cols, k_cols)], w_sem.at[1]),
        pltpu.make_async_copy(wv_ref, w.at[:, pl.ds(q_cols + k_cols, k_cols)], w_sem.at[2]),
    ]
    for load in loads:
        load.start()
    await_plane(barrier, z)
    for load in loads:
        load.wait()
    sends = Sends()
    tile = 512

    def row_ds(xr, h=None):
        if h is None:
            return pl.ds(pl.multiple_of(xr * rows, rows), rows)
        return pl.ds(pl.multiple_of(xr * rows + h * half, half), half)

    def compute(zr):
        lhs = jnp.concatenate(
            [
                grads_ref[pl.ds(pl.multiple_of(i * NZ * rows + zr * rows, rows), rows), :]
                for i in range(NX)
            ],
            axis=0,
        )

        @pl.loop(0, width // tile)
        def _(j):
            at = pl.ds(pl.multiple_of(j * tile, tile), tile)
            p[zr, :, at] = lax.dot_general(
                lhs, w[at, :], (((1,), (1,)), ((), ())), preferred_element_type=jnp.float32
            ).astype(jnp.bfloat16)

    def far_exists(zr):
        return ((zr < z) & (z < NZ - 1)) | ((zr > z) & (z > 0))

    def way(zr):
        return jnp.where(zr > z, 1, 0)

    def nearer(zr):
        return tp_of(x, jnp.where(zr > z, z + 1, z - 1))

    def step1(k, zr, cols):
        for direction, to in ((0, xm), (1, xp)):
            sends.start(
                send_to(
                    p.at[zr, row_ds(xo, direction), cols],
                    got_opp.at[direction, zr, :, cols],
                    s1.at[direction, k],
                    r1.at[direction, k],
                    tp_of(to, z),
                )
            )

    def step2(k, zr, cols):
        for direction, to in ((0, xm), (1, xp)):
            land = got_opp.at[direction, zr, :, cols]
            send_to(land, land, s1.at[direction, k], r1.at[direction, k], tp_of(to, z)).wait_recv()
            at = row_ds(to, direction)
            p[zr, at, cols] = (
                p[zr, at, cols].astype(jnp.float32)
                + got_opp[direction, zr, :, cols].astype(jnp.float32)
            ).astype(jnp.bfloat16)
            sends.start(
                send_to(
                    p.at[zr, row_ds(to), cols],
                    got_x.at[direction, zr, :, cols],
                    s2.at[direction, k],
                    r2.at[direction, k],
                    tp_of(to, z),
                )
            )

    def x_sum(k, zr, cols):
        for direction, to in ((0, xm), (1, xp)):
            land = got_x.at[direction, zr, :, cols]
            send_to(land, land, s2.at[direction, k], r2.at[direction, k], tp_of(to, z)).wait_recv()
        return (
            p[zr, row_ds(x), cols].astype(jnp.float32)
            + got_x[0, zr, :, cols].astype(jnp.float32)
            + got_x[1, zr, :, cols].astype(jnp.float32)
        )

    def z_wait_b(d, zr):
        land = got_zb.at[d, zr]
        send_to(land, land, szb.at[0], rzb.at[d, zr], tp_of(xp, z)).wait_recv()

    def z_wait_a(d, zr):
        land = got_za.at[d, zr]
        send_to(land, land, sza.at[0], rza.at[d, zr], tp_of(xp, z)).wait_recv()

    def step3(k, zr, far):
        copy = send_to(
            p.at[zr, row_ds(x), b_cols], got_zb.at[way(zr), zr], szb.at[k],
            rzb.at[way(zr), zr], nearer(zr),
        )

        def run():
            value = x_sum(k, zr, b_cols)
            if far:
                z_wait_b(way(zr), zr)
                value = value + got_zb[way(zr), zr].astype(jnp.float32)
            p[zr, row_ds(x), b_cols] = value.astype(jnp.bfloat16)
            copy.start()

        if far:
            pl.when(far_exists(zr))(run)
            sends.started.append((copy, None))
        else:
            pl.when(jnp.logical_not(far_exists(zr)))(run)

    def line_a(k, zr, far):
        copy = send_to(
            p.at[zr, :, a_cols], got_za.at[way(zr), zr], sza.at[k],
            rza.at[way(zr), zr], nearer(zr),
        )

        def run():
            if far:
                z_wait_a(way(zr), zr)
                p[zr, :, a_cols] = (
                    p[zr, :, a_cols].astype(jnp.float32)
                    + got_za[way(zr), zr].astype(jnp.float32)
                ).astype(jnp.bfloat16)
            copy.start()

        if far:
            pl.when(far_exists(zr))(run)
            sends.started.append((copy, None))
        else:
            pl.when(jnp.logical_not(far_exists(zr)))(run)

    compute(zs[0])
    step1(0, zs[0], b_cols)
    line_a(0, zs[0], False)
    compute(zs[1])
    step1(1, zs[1], b_cols)
    line_a(1, zs[1], False)
    step2(0, zs[0], b_cols)
    line_a(0, zs[0], True)
    compute(zs[2])
    step1(2, zs[2], b_cols)
    line_a(2, zs[2], False)
    step2(1, zs[1], b_cols)
    line_a(1, zs[1], True)
    step3(0, zs[0], False)
    compute(z)
    step1(3, z, b_cols)
    step2(2, zs[2], b_cols)
    line_a(2, zs[2], True)
    step3(1, zs[1], False)
    step3(0, zs[0], True)
    step2(3, z, b_cols)
    step3(2, zs[2], False)

    for d, there in ((0, z < NZ - 1), (1, z > 0)):

        @pl.when(there)
        def _(d=d):
            z_wait_a(d, z)
            p[z, :, a_cols] = (
                p[z, :, a_cols].astype(jnp.float32) + got_za[d, z].astype(jnp.float32)
            ).astype(jnp.bfloat16)

    step1(4, z, a_cols)
    step3(1, zs[1], True)
    step2(4, z, a_cols)
    step3(2, zs[2], True)
    total[:, b_cols] = x_sum(3, z, b_cols)
    for d, there in ((0, z < NZ - 1), (1, z > 0)):

        @pl.when(there)
        def _(d=d):
            z_wait_b(d, z)
            total[:, b_cols] = total[:, b_cols] + got_zb[d, z].astype(jnp.float32)

    total[:, a_cols] = x_sum(4, z, a_cols)
    values = tokens_ref[...].astype(jnp.float32)
    inv = lax.rsqrt(jnp.mean(values * values, axis=1, keepdims=True) + EPS)
    upper = total[...] * gain_ref[...]
    xhat = values * inv
    out_ref[...] = (
        inv * (upper - xhat * jnp.mean(upper * xhat, axis=1, keepdims=True))
    ).astype(jnp.bfloat16)
    sends.finish()


def product_scatter_call(tokens, gain, grads, wq, wk, wv):
    rows, width = tokens.shape
    cols = wq.shape[1] + 2 * wk.shape[1]
    a_width = A_TILES * 128
    vmem = pl.BlockSpec(memory_space=pltpu.VMEM)
    any_space = pl.BlockSpec(memory_space=pl.ANY)
    dma = pltpu.SemaphoreType.DMA
    return pl.pallas_call(
        product_scatter,
        out_shape=jax.ShapeDtypeStruct((rows, width), jnp.bfloat16),
        in_specs=[vmem, vmem, vmem, any_space, any_space, any_space],
        out_specs=vmem,
        scratch_shapes=[
            pltpu.VMEM((NZ, NX * rows, width), jnp.bfloat16),
            pltpu.VMEM((width, cols), jnp.bfloat16),
            pltpu.VMEM((rows, width), jnp.float32),
            pltpu.VMEM((2, NZ, rows // 2, width), jnp.bfloat16),
            pltpu.VMEM((2, NZ, rows, width), jnp.bfloat16),
            pltpu.VMEM((2, NZ, NX * rows, a_width), jnp.bfloat16),
            pltpu.VMEM((2, NZ, rows, width - a_width), jnp.bfloat16),
            dma((3,)),
            dma((2, NZ + 1)),
            dma((2, NZ + 1)),
            dma((2, NZ + 1)),
            dma((2, NZ + 1)),
            dma((NZ,)),
            dma((2, NZ)),
            dma((NZ,)),
            dma((2, NZ)),
        ],
        compiler_params=pltpu.CompilerParams(
            collective_id=1, has_side_effects=True, vmem_limit_bytes=48 * 1024 * 1024
        ),
    )(tokens, gain, grads, wq, wk, wv)


def shifted(block, axis, distance):
    devices = range(lax.axis_size(axis))
    route = [(i - distance, i) for i in devices if i - distance in devices]
    return lax.ppermute(block, axis, route)


def block_grads(query_blk, grad_blk, key_blk, value_blk, query_pos, key_pos):
    row_count = query_blk.shape[0]
    key_span = key_blk.shape[0]
    kv_heads = key_blk.shape[1] // HEAD_SIZE
    groups = query_blk.shape[1] // key_blk.shape[1]
    query_four = query_blk.reshape(row_count, kv_heads, groups, HEAD_SIZE)
    grad_four = grad_blk.reshape(row_count, kv_heads, groups, HEAD_SIZE)
    key_three = key_blk.reshape(key_span, kv_heads, HEAD_SIZE)
    value_three = value_blk.reshape(key_span, kv_heads, HEAD_SIZE)
    raw = jnp.einsum("qkgd,skd->kgqs", query_four, key_three, preferred_element_type=jnp.float32)
    bent = jnp.tanh(raw * SCALE / CAP)
    capped = CAP * bent
    valid = (
        (key_pos[None, :] <= query_pos[:, None])
        & (key_pos[None, :] > query_pos[:, None] - WINDOW)
        & (key_pos[None, :] >= 0)
    )
    expo = jnp.where(valid, jnp.exp(capped), 0.0)
    probs = expo / jnp.sum(expo, axis=-1, keepdims=True)
    d_probs = jnp.einsum(
        "qkgd,skd->kgqs", grad_four, value_three, preferred_element_type=jnp.float32
    )
    delta = jnp.sum(probs * d_probs, axis=-1, keepdims=True)
    d_raw = (probs * (d_probs - delta) * (1.0 - bent * bent) * SCALE).astype(jnp.bfloat16)
    probs_low = probs.astype(jnp.bfloat16)
    grad_query = jnp.einsum(
        "kgqs,skd->qkgd", d_raw, key_three, preferred_element_type=jnp.float32
    ).reshape(row_count, kv_heads * groups * HEAD_SIZE)
    grad_key = jnp.einsum(
        "kgqs,qkgd->skd", d_raw, query_four, preferred_element_type=jnp.float32
    ).reshape(key_span, kv_heads * HEAD_SIZE)
    grad_value = jnp.einsum(
        "kgqs,qkgd->skd", probs_low, grad_four, preferred_element_type=jnp.float32
    ).reshape(key_span, kv_heads * HEAD_SIZE)
    return (grad_query, grad_key, grad_value)


def on_device(tokens, norm_gain, query_weight, key_matrix, value_matrix, output_grad):
    local_rows = output_grad.shape[0]
    query_cols = query_weight.shape[1]
    key_cols = key_matrix.shape[1]
    reach = WINDOW - local_rows
    key_span = WINDOW + local_rows
    gain = norm_gain.reshape(1, -1)
    joined = gather_project_call(tokens, gain, query_weight, key_matrix, value_matrix)
    query_own = joined[:, :query_cols]
    key_own = joined[:, query_cols : query_cols + key_cols]
    value_own = joined[:, query_cols + key_cols :]
    near_key, near_value = shifted((key_own, value_own), "seq", 1)
    far_key, far_value = shifted(
        (key_own[local_rows - reach :], value_own[local_rows - reach :]), "seq", 2
    )
    all_key = jnp.concatenate([far_key, near_key, key_own], axis=0)
    all_value = jnp.concatenate([far_value, near_value, value_own], axis=0)
    anchor = lax.axis_index("seq") * local_rows
    query_pos = anchor + jnp.arange(local_rows, dtype=jnp.int32)
    key_pos = anchor - WINDOW + jnp.arange(key_span, dtype=jnp.int32)
    grad_query, acc_key, acc_value = block_grads(
        query_own, output_grad, all_key, all_value, query_pos, key_pos
    )
    far_back_key, far_back_value = shifted((acc_key[:reach], acc_value[:reach]), "seq", -2)
    back_key, back_value = shifted(
        (acc_key[reach : reach + local_rows], acc_value[reach : reach + local_rows]), "seq", -1
    )
    own_gkey = acc_key[reach + local_rows :] + back_key
    own_gvalue = acc_value[reach + local_rows :] + back_value
    own_gkey = own_gkey.at[local_rows - reach :].add(far_back_key)
    own_gvalue = own_gvalue.at[local_rows - reach :].add(far_back_value)
    grads = jnp.concatenate([grad_query, own_gkey, own_gvalue], axis=1).astype(jnp.bfloat16)
    return product_scatter_call(tokens, gain, grads, query_weight, key_matrix, value_matrix)


def solution(mesh):
    tp, both = "tp", ("seq", "tp")
    in_specs = (P(both, None), P(), P(None, tp), P(None, tp), P(None, tp), P("seq", tp))
    return jax.shard_map(
        on_device, mesh=mesh, in_specs=in_specs, out_specs=P(both, None), check_vma=False
    )
```

time: 297 us -> 163 us (0.55)
  waiting for transfers between devices: 215 us -> 8.44 us
  Pallas kernels: 0 us -> 91.7 us
  matrix products: 26.6 us -> 6.88 us
  local copies, waits for them, and re-layouts: 0.34 us -> 14.5 us
  between operations: 13.4 us -> 0.41 us
    all_gather x1 -> x0, waiting for transfers between devices: 116 us -> none  [on_device(): lax.all_gather(tokens, TP, axis=0, tiled=True)]
    pallas_call x0 -> x2, Pallas kernels: none -> 91.7 us  [the longest x1 47.1 us: gather_project_call(): pl.pallas_call(gather_project, out_shape=jax.ShapeDtypeStruct((rows * NX...]
    reduce_scatter x2 -> x0, waiting for transfers between devices: 89 us -> none  [sum_by_axis(): so_far = lax.psum_scatter(so_far, axis, scatter_dimension=0, tiled=True)]
    dot_general x6 -> x0, matrix products: 20.3 us -> none  [the longest x3 14.2 us: row_product(): lax.dot_general(grad_rows, weight, (((1,), (1,)), ((), ())), preferred_el...]
    unnamed x14 -> x39, local copies, waits for them, and re-layouts: 0.28 us -> 8.88 us
    reduce_sum x3 -> x0, other arithmetic: 4.88 us -> none  [the longest x1 3.48 us: normalize_project(): jnp.mean(float_values * float_values, axis=1, keepdims=True) + EPS]
  transfers between devices with their start and end apart: 11 -> 8, of which waited for: 6 -> 3; matrix products, arithmetic and copies ran while one was open for 5% -> 7% of each run, Pallas kernels for 0% -> 0%
where the time goes in v1:
time: 163 us; the launch traced here: 162 us
  Pallas kernels  91.7 us (56%)
  starting transfers between devices  33.2 us (20%)
  local copies, waits for them, and re-layouts  14.5 us (9%)
  waiting for transfers between devices  8.44 us (5%)
  other arithmetic  7.2 us (4%)
  matrix products  6.88 us (4%)
    pallas_call x1, Pallas kernels, gather_project_call(): pl.pallas_call(gather_project, out_shape=jax.ShapeDtypeStruct((rows * NX...  47.1 us
    pallas_call x1, Pallas kernels, product_scatter_call(): pl.pallas_call(product_scatter, out_shape=jax.ShapeDtypeStruct((rows, wid...  44.6 us
    ppermute x8, starting transfers between devices, shifted(): return lax.ppermute(block, axis, route)  33.2 us
    unnamed x39, local copies, waits for them, and re-layouts  8.88 us
    ppermute x8, waiting for transfers between devices, shifted(): return lax.ppermute(block, axis, route)  8.44 us
  transfers between devices with their start and end apart: 8, of which 3 were waited for; matrix products, arithmetic and copies ran while one was open for 7% of the time, Pallas kernels for 0%

profile of v1, /device:TPU:24, one launch (start us, length us, event | category | flops | bytes accessed | tf_op | source)
XLA Modules:
  0.0 162.3 jit_solution(5185066079363601230)
XLA Ops:
  0.0 0.7 reshape.131.gain_ref
  0.7 0.0 copy-start
  0.8 1.7 %copy-done = bf16[4608,256]{1,0:T(8,128)(2,1)S(1)} copy-done((bf16[4608,256]{1,0:T(8,128)(2,1)S(1)}, bf16[4608,256]{1,0:T(8,128)(2,1)}, u32[]{:S(2)}) %copy-start) | copy-done | bytes 2359320
  2.4 1.3 copy-done.2
  3.7 1.3 copy-done.4
  5.0 1.0 copy-done.6
  5.9 47.1 %shard_map.64 = bf16[512,512]{1,0:T(8,128)(2,1)S(1)} custom-call(bf16[32,4608]{1,0:T(8,128)(2,1)S(1)} %copy-done.6, f32[1,4608]{1,0:T(1,128)S(1)} %reshape.131.gain_ref, bf16[4608,256]{1,0:T(8,128)(2,1)S(1)} %copy-done, bf16[4608,128]{1,0:T(8,128)(2,1)S(1)} %copy-done.2, bf16[4608,128]{1,0:T(8,128)(2,1)S(1)} %copy-done.4), custom_call_target="tpu_custom_call" | custom-call | tf_op jit(solution)/shard_map/pallas_call | solution.py:213
  53.0 0.0 copy-done.8
  53.0 7.7 %collective-permute-start.2 = (bf16[128,128]{1,0:T(8,128)(2,1)S(1)}, bf16[128,128]{1,0:T(8,128)(2,1)S(1)}, u32[]{:S(2)}, u32[]{:S(2)}) collective-permute-start(bf16[128,128]{1,0:T(8,128)(2,1)S(1)} %get-tuple-element.29), channel_id=1, source_target_pairs={{0,32},{16,48},{32,64},{48,80},{64,96},{80,112},{96,128},{112,144}... | collective-permute-start | bytes 98312 | tf_op jit(solution)/shard_map/ppermute | solution.py:476
  60.7 1.9 %collective-permute-start = (bf16[128,128]{1,0:T(8,128)(2,1)S(1)}, bf16[128,128]{1,0:T(8,128)(2,1)S(1)}, u32[]{:S(2)}, u32[]{:S(2)}) collective-permute-start(bf16[128,128]{1,0:T(8,128)(2,1)S(1)} %get-tuple-element.30), channel_id=1, source_target_pairs={{0,32},{16,48},{32,64},{48,80},{64,96},{80,112},{96,128},{112,144}... | collective-permute-start | bytes 98312 | tf_op jit(solution)/shard_map/ppermute | solution.py:476
  62.7 0.0 copy-start.12
  62.7 1.9 %collective-permute-start.3 = (bf16[512,128]{1,0:T(8,128)(2,1)S(1)}, bf16[512,128]{1,0:T(8,128)(2,1)S(1)}, u32[]{:S(2)}, u32[]{:S(2)}) collective-permute-start(bf16[512,128]{1,0:T(8,128)(2,1)S(1)} %get-tuple-element.31), channel_id=1, source_target_pairs={{0,16},{16,32},{32,48},{48,64},{64,80},{80,96},{96,112},{112,128},... | collective-permute-start | bytes 393224 | tf_op jit(solution)/shard_map/ppermute | solution.py:476
  64.6 1.9 %collective-permute-start.1 = (bf16[512,128]{1,0:T(8,128)(2,1)S(1)}, bf16[512,128]{1,0:T(8,128)(2,1)S(1)}, u32[]{:S(2)}, u32[]{:S(2)}) collective-permute-start(bf16[512,128]{1,0:T(8,128)(2,1)S(1)} %get-tuple-element.32), channel_id=1, source_target_pairs={{0,16},{16,32},{32,48},{48,64},{64,80},{80,96},{96,112},{112,128},... | collective-permute-start | bytes 393224 | tf_op jit(solution)/shard_map/ppermute | solution.py:476
  66.6 0.9 and_and_fusion
  67.6 0.0 copy-done.14
  67.6 0.1 copy.29
  67.7 0.1 copy.28
  67.9 3.9 %collective-permute-done = bf16[128,128]{1,0:T(8,128)(2,1)S(1)} collective-permute-done((bf16[128,128]{1,0:T(8,128)(2,1)S(1)}, bf16[128,128]{1,0:T(8,128)(2,1)S(1)}, u32[]{:S(2)}, u32[]{:S(2)}) %collective-permute-start) | collective-permute-done | bytes 32800 | tf_op jit(solution)/shard_map/ppermute | solution.py:476
  71.8 4.2 %collective-permute-done.1 = bf16[512,128]{1,0:T(8,128)(2,1)S(1)} collective-permute-done((bf16[512,128]{1,0:T(8,128)(2,1)S(1)}, bf16[512,128]{1,0:T(8,128)(2,1)S(1)}, u32[]{:S(2)}, u32[]{:S(2)}) %collective-permute-start.1) | collective-permute-done | bytes 131104 | tf_op jit(solution)/shard_map/ppermute | solution.py:476
  76.0 1.7 %fusion.5 = (f32[2,512]{1,0:T(2,128)S(1)}, f32[1152,512,2]{1,0,2:T(8,128)S(1)}) fusion(pred[512,1152]{0,1:T(8,128)(4,1)S(1)} %and_and_fusion, bf16[512,2,128]{0,2,1:T(8,128)(2,1)S(1)} %bitcast.97, bf16[512,128]{1,0:T(8,128)(2,1)S(1)} %get-tuple-element.32, bf16[512,128]{1,0:T(8,128)(2,1)S(1)} %collective-permute-done.1, ...), kind=kOutput, calls=%fused_computation.10 | convolution fusion | flops 307592192 | bytes 5869568 | tf_op jit(solution)/shard_map/qkgd,skd->kgqs/dot_general | solution.py:488
  77.7 0.0 copy-done.12
  77.7 0.0 copy-done.17
  77.7 0.0 copy-done.15
  77.7 1.4 convolution_bitcast_fusion
  79.2 0.0 copy-start.11
  79.2 0.8 slice_bitcast_fusion
  80.0 0.6 slice_bitcast_fusion.4
  80.6 0.0 collective-permute-done.2
  80.6 0.0 copy-done.11
  80.6 0.0 collective-permute-done.3
  80.6 1.7 %fusion.2 = (f32[2,512]{1,0:T(2,128)S(1)}, f32[1152,512,2]{1,0,2:T(8,128)S(1)}) fusion(f32[2,512]{1,0:T(2,128)S(1)} %get-tuple-element.33, f32[1152,512,2]{1,0,2:T(8,128)S(1)} %get-tuple-element.34, pred[512,1152]{0,1:T(8,128)(4,1)S(1)} %and_and_fusion, bf16[512,2,128]{0,2,1:T(8,128)(2,1)S(1)} %bitcast.101, bf16[512,128]{1,0:T(8,128)(2,1)S(1)} %get-tuple-element.31, ...), kind=kOutput, calls=%fused_computation.7 | convolution fusion | flops 308771840 | bytes 10592256 | tf_op jit(solution)/shard_map/qkgd,skd->kgqs/dot_general | solution.py:498
  82.3 0.0 copy-start.13
  82.4 0.0 copy-start.16
  82.4 0.0 copy-start.18
  82.4 2.2 %fusion.6 = bf16[2,512,1152]{1,2,0:T(8,128)(2,1)S(1)} fusion(f32[1152,512,2]{1,0,2:T(8,128)S(1)} %get-tuple-element.34, f32[1152,512,2]{1,0,2:T(8,128)S(1)} %get-tuple-element.36, f32[2,512]{1,0:T(2,128)S(1)} %get-tuple-element.35, f32[2,512]{1,0:T(2,128)S(1)} %get-tuple-element.33, pred[512,1152]{0,1:T(8,128)(4,1)S(1)} %and_and_fusion), kind=kLoop, calls=%fused_computation.13 | loop fusion | flops 11796480 | bytes 12394496 | tf_op jit(solution)/shard_map/reshape.59
  84.6 0.8 convolution_bitcast_fusion.1
  85.4 0.0 copy-start.10
  85.4 0.0 copy-start.1
  85.4 0.0 copy-start.3
  85.4 0.6 slice_bitcast_fusion.5
  86.1 0.7 slice_bitcast_fusion.2
  86.8 7.6 %collective-permute-start.7 = (f32[128,128]{1,0:T(8,128)}, f32[128,128]{1,0:T(8,128)}, u32[]{:S(2)}, u32[]{:S(2)}) collective-permute-start(f32[128,128]{1,0:T(8,128)} %slice_bitcast_fusion.4), channel_id=1, source_target_pairs={{32,0},{48,16},{64,32},{80,48},{96,64},{112,80},{128,96},{144,112}... | collective-permute-start | bytes 196616 | tf_op jit(solution)/shard_map/ppermute | solution.py:476
  94.4 1.9 %collective-permute-start.6 = (f32[512,128]{1,0:T(8,128)}, f32[512,128]{1,0:T(8,128)}, u32[]{:S(2)}, u32[]{:S(2)}) collective-permute-start(f32[512,128]{1,0:T(8,128)} %slice_bitcast_fusion), channel_id=1, source_target_pairs={{16,0},{32,16},{48,32},{64,48},{80,64},{96,80},{112,96},{128,112},... | collective-permute-start | bytes 786440 | tf_op jit(solution)/shard_map/ppermute | solution.py:476
  96.4 3.2 %collective-permute-start.4 = (f32[512,128]{1,0:T(8,128)}, f32[512,128]{1,0:T(8,128)}, u32[]{:S(2)}, u32[]{:S(2)}) collective-permute-start(f32[512,128]{1,0:T(8,128)} %slice_bitcast_fusion.2), channel_id=1, source_target_pairs={{16,0},{32,16},{48,32},{64,48},{80,64},{96,80},{112,96},{128,112},... | collective-permute-start | bytes 786440 | tf_op jit(solution)/shard_map/ppermute | solution.py:476
  99.6 0.0 copy-done.13
  99.6 0.0 copy-done.16
  99.6 0.0 copy-done.18
  99.6 1.3 convolution_convert_fusion
  100.9 1.8 %copy.25 = bf16[512,256]{1,0:T(8,128)(2,1)} copy(bf16[512,256]{0,1:T(8,128)(2,1)} %bitcast.99) | data formatting | bytes 524288 | tf_op jit(solution)/shard_map/reshape | solution.py:506
  102.7 7.0 %collective-permute-start.5 = (f32[128,128]{1,0:T(8,128)}, f32[128,128]{1,0:T(8,128)S(1)}, u32[]{:S(2)}, u32[]{:S(2)}) collective-permute-start(f32[128,128]{1,0:T(8,128)} %slice_bitcast_fusion.5), channel_id=1, source_target_pairs={{32,0},{48,16},{64,32},{80,48},{96,64},{112,80},{128,96},{144,112}... | collective-permute-start | bytes 196616 | tf_op jit(solution)/shard_map/ppermute | solution.py:476
  109.7 0.0 collective-permute-done.6
  109.7 1.1 fusion.15
  110.8 0.0 collective-permute-done.4
  110.8 1.1 fusion.16
  111.8 0.0 collective-permute-done.7
  111.8 0.9 fusion.17
  112.7 0.2 collective-permute-done.5
  113.0 1.0 pad_maximum_fusion.grads_ref
  114.0 0.0 copy-start.5
  114.0 1.3 copy-done.5
  115.3 1.0 copy-done.7
  116.3 0.7 copy-done.9
  117.0 44.6 %shard_map.65 = bf16[32,4608]{1,0:T(8,128)(2,1)S(1)} custom-call(bf16[32,4608]{1,0:T(8,128)(2,1)S(1)} %copy-done.7, f32[1,4608]{1,0:T(1,128)S(1)} %copy-done.9, bf16[512,512]{1,0:T(8,128)(2,1)S(1)} %pad_maximum_fusion.grads_ref, bf16[4608,256]{1,0:T(8,128)(2,1)S(1)} %copy-done.1, bf16[4608,128]{1,0:T(8,128)(2,1)S(1)} %copy-done.3, ...), custom_call_target="tpu_custom_call" | custom-call | tf_op jit(solution)/shard_map/pallas_call | solution.py:444
  161.6 0.7 copy.33
  (21 shorter events, 0.1 us)
Async XLA Ops:
  0.7 1.7 %copy-start = (bf16[4608,256]{1,0:T(8,128)(2,1)S(1)}, bf16[4608,256]{1,0:T(8,128)(2,1)}, u32[]{:S(2)}) copy-start(bf16[4608,256]{1,0:T(8,128)(2,1)} %wq_ref.3) | copy-start | bytes 7077892
  2.4 1.3 copy-start.2
  3.7 1.3 copy-start.4
  5.0 1.0 copy-start.6
  5.9 47.1 %copy-start.8 = (f32[1,4608]{1,0:T(1,128)}, f32[1,4608]{1,0:T(1,128)S(1)}, u32[]{:S(2)}) copy-start(f32[1,4608]{1,0:T(1,128)S(1)} %reshape.131.gain_ref) | copy-start | bytes 55300
  5.9 61.6 %copy-start.14 = (bf16[512,256]{1,0:T(8,128)(2,1)S(1)}, bf16[512,256]{1,0:T(8,128)(2,1)}, u32[]{:S(2)}) copy-start(bf16[512,256]{1,0:T(8,128)(2,1)} %param.15) | copy-start | bytes 786436
  53.0 27.6 %collective-permute-start.2 = (bf16[128,128]{1,0:T(8,128)(2,1)S(1)}, bf16[128,128]{1,0:T(8,128)(2,1)S(1)}, u32[]{:S(2)}, u32[]{:S(2)}) collective-permute-start(bf16[128,128]{1,0:T(8,128)(2,1)S(1)} %get-tuple-element.29), channel_id=1, source_target_pairs={{0,32},{16,48},{32,64},{48,80},{64,96},{80,112},{96,128},{112,144}... | collective-permute-start | bytes 98312 | tf_op jit(solution)/shard_map/ppermute | solution.py:476
  60.7 11.1 %collective-permute-start = (bf16[128,128]{1,0:T(8,128)(2,1)S(1)}, bf16[128,128]{1,0:T(8,128)(2,1)S(1)}, u32[]{:S(2)}, u32[]{:S(2)}) collective-permute-start(bf16[128,128]{1,0:T(8,128)(2,1)S(1)} %get-tuple-element.30), channel_id=1, source_target_pairs={{0,32},{16,48},{32,64},{48,80},{64,96},{80,112},{96,128},{112,144}... | collective-permute-start | bytes 98312 | tf_op jit(solution)/shard_map/ppermute | solution.py:476
  62.7 15.0 %copy-start.12 = (bf16[512,128]{1,0:T(8,128)(2,1)}, bf16[512,128]{1,0:T(8,128)(2,1)S(1)}, u32[]{:S(2)}) copy-start(bf16[512,128]{1,0:T(8,128)(2,1)S(1)} %get-tuple-element.32) | copy-start | bytes 393220
  62.7 17.9 %collective-permute-start.3 = (bf16[512,128]{1,0:T(8,128)(2,1)S(1)}, bf16[512,128]{1,0:T(8,128)(2,1)S(1)}, u32[]{:S(2)}, u32[]{:S(2)}) collective-permute-start(bf16[512,128]{1,0:T(8,128)(2,1)S(1)} %get-tuple-element.31), channel_id=1, source_target_pairs={{0,16},{16,32},{32,48},{48,64},{64,80},{80,96},{96,112},{112,128},... | collective-permute-start | bytes 393224 | tf_op jit(solution)/shard_map/ppermute | solution.py:476
  64.6 11.4 %collective-permute-start.1 = (bf16[512,128]{1,0:T(8,128)(2,1)S(1)}, bf16[512,128]{1,0:T(8,128)(2,1)S(1)}, u32[]{:S(2)}, u32[]{:S(2)}) collective-permute-start(bf16[512,128]{1,0:T(8,128)(2,1)S(1)} %get-tuple-element.32), channel_id=1, source_target_pairs={{0,16},{16,32},{32,48},{48,64},{64,80},{80,96},{96,112},{112,128},... | collective-permute-start | bytes 393224 | tf_op jit(solution)/shard_map/ppermute | solution.py:476
  71.8 5.9 %copy-start.17 = (bf16[128,128]{1,0:T(8,128)(2,1)}, bf16[128,128]{1,0:T(8,128)(2,1)S(1)}, u32[]{:S(2)}) copy-start(bf16[128,128]{1,0:T(8,128)(2,1)S(1)} %collective-permute-done) | copy-start | bytes 98308
  76.0 1.7 %copy-start.15 = (bf16[512,128]{1,0:T(8,128)(2,1)}, bf16[512,128]{1,0:T(8,128)(2,1)S(1)}, u32[]{:S(2)}) copy-start(bf16[512,128]{1,0:T(8,128)(2,1)S(1)} %collective-permute-done.1) | copy-start | bytes 393220
  79.2 1.4 copy-start.11
  82.3 17.2 %copy-start.13 = (bf16[512,128]{1,0:T(8,128)(2,1)S(1)}, bf16[512,128]{1,0:T(8,128)(2,1)}, u32[]{:S(2)}) copy-start(bf16[512,128]{1,0:T(8,128)(2,1)} %copy-done.12) | copy-start | bytes 393220
  82.4 17.2 %copy-start.16 = (bf16[512,128]{1,0:T(8,128)(2,1)S(1)}, bf16[512,128]{1,0:T(8,128)(2,1)}, u32[]{:S(2)}) copy-start(bf16[512,128]{1,0:T(8,128)(2,1)} %copy-done.15) | copy-start | bytes 393220
  82.4 17.2 %copy-start.18 = (bf16[128,128]{1,0:T(8,128)(2,1)S(1)}, bf16[128,128]{1,0:T(8,128)(2,1)}, u32[]{:S(2)}) copy-start(bf16[128,128]{1,0:T(8,128)(2,1)} %copy-done.17) | copy-start | bytes 98308
  85.4 15.5 %copy-start.10 = (f32[1152,1,128]{2,0,1:T(8,128)}, f32[1152,1,128]{2,0,1:T(8,128)S(1)}, u32[]{:S(2)}) copy-start(f32[1152,1,128]{2,0,1:T(8,128)S(1)} %convolution_bitcast_fusion.1) | copy-start | bytes 1769476
  85.4 28.6 %copy-start.1 = (bf16[4608,256]{1,0:T(8,128)(2,1)S(1)}, bf16[4608,256]{1,0:T(8,128)(2,1)}, u32[]{:S(2)}) copy-start(bf16[4608,256]{1,0:T(8,128)(2,1)} %wq_ref.3) | copy-start | bytes 7077892
  85.4 28.6 %copy-start.3 = (bf16[4608,128]{1,0:T(8,128)(2,1)S(1)}, bf16[4608,128]{1,0:T(8,128)(2,1)}, u32[]{:S(2)}) copy-start(bf16[4608,128]{1,0:T(8,128)(2,1)} %wk_ref.3) | copy-start | bytes 3538948
  86.8 25.0 %collective-permute-start.7 = (f32[128,128]{1,0:T(8,128)}, f32[128,128]{1,0:T(8,128)}, u32[]{:S(2)}, u32[]{:S(2)}) collective-permute-start(f32[128,128]{1,0:T(8,128)} %slice_bitcast_fusion.4), channel_id=1, source_target_pairs={{32,0},{48,16},{64,32},{80,48},{96,64},{112,80},{128,96},{144,112}... | collective-permute-start | bytes 196616 | tf_op jit(solution)/shard_map/ppermute | solution.py:476
  94.4 15.3 %collective-permute-start.6 = (f32[512,128]{1,0:T(8,128)}, f32[512,128]{1,0:T(8,128)}, u32[]{:S(2)}, u32[]{:S(2)}) collective-permute-start(f32[512,128]{1,0:T(8,128)} %slice_bitcast_fusion), channel_id=1, source_target_pairs={{16,0},{32,16},{48,32},{64,48},{80,64},{96,80},{112,96},{128,112},... | collective-permute-start | bytes 786440 | tf_op jit(solution)/shard_map/ppermute | solution.py:476
  96.4 14.4 %collective-permute-start.4 = (f32[512,128]{1,0:T(8,128)}, f32[512,128]{1,0:T(8,128)}, u32[]{:S(2)}, u32[]{:S(2)}) collective-permute-start(f32[512,128]{1,0:T(8,128)} %slice_bitcast_fusion.2), channel_id=1, source_target_pairs={{16,0},{32,16},{48,32},{64,48},{80,64},{96,80},{112,96},{128,112},... | collective-permute-start | bytes 786440 | tf_op jit(solution)/shard_map/ppermute | solution.py:476
  102.7 10.3 %collective-permute-start.5 = (f32[128,128]{1,0:T(8,128)}, f32[128,128]{1,0:T(8,128)S(1)}, u32[]{:S(2)}, u32[]{:S(2)}) collective-permute-start(f32[128,128]{1,0:T(8,128)} %slice_bitcast_fusion.5), channel_id=1, source_target_pairs={{32,0},{48,16},{64,32},{80,48},{96,64},{112,80},{128,96},{144,112}... | collective-permute-start | bytes 196616 | tf_op jit(solution)/shard_map/ppermute | solution.py:476
  114.0 1.3 copy-start.5
  115.3 1.0 copy-start.7
  116.3 0.7 copy-start.9

commit v2 on v1

v2 whole, which is shorter than its diff:
```python
import jax
import jax.numpy as jnp
from jax import lax
from jax.experimental import pallas as pl
from jax.experimental.pallas import tpu as pltpu
from jax.sharding import PartitionSpec as P

HEAD_SIZE = 128
WINDOW = 640
SCALE = 1.0 / 12.0
CAP = 50.0
EPS = 1e-06
MESH = pl.DeviceIdType.MESH
NX = 4
NZ = 4
A_TILES = 8


def place():
    t = lax.axis_index("tp")
    return t // NZ, t % NZ


def near_to_far(z):
    def high(q):
        return (q, 5 - q, jnp.int32(1), jnp.int32(0))

    up = high(z)
    low = high(3 - z)
    return [jnp.where(z >= 2, u, 3 - v) for u, v in zip(up, low)]


def send_to(src, dst, send_sem, recv_sem, tp):
    return pltpu.make_async_remote_copy(
        src_ref=src,
        dst_ref=dst,
        send_sem=send_sem,
        recv_sem=recv_sem,
        device_id={"tp": tp},
        device_id_type=MESH,
    )


def tp_of(x, z):
    return x * NZ + z


def send_along(src, dst, send_sem, recv_sem, seq):
    return pltpu.make_async_remote_copy(
        src_ref=src,
        dst_ref=dst,
        send_sem=send_sem,
        recv_sem=recv_sem,
        device_id={"seq": seq},
        device_id_type=MESH,
    )


def greet_partners(x, z, s, blocks):
    barrier = pltpu.get_barrier_semaphore()

    def greet(device):
        pl.semaphore_signal(barrier, inc=1, device_id=device, device_id_type=MESH)

    greet({"tp": tp_of((x + 1) % NX, z)})
    greet({"tp": tp_of((x + 3) % NX, z)})
    pl.when(z > 0)(lambda: greet({"tp": tp_of(x, z - 1)}))
    pl.when(z < NZ - 1)(lambda: greet({"tp": tp_of(x, z + 1)}))
    count = jnp.where((z == 0) | (z == NZ - 1), 3, 4)
    for step in (-2, -1, 1, 2):
        there = (s + step >= 0) & (s + step < blocks)
        pl.when(there)(lambda step=step: greet({"seq": s + step}))
        count = count + jnp.where(there, 1, 0)
    return barrier, count


class Sends:
    def __init__(self):
        self.started = []

    def start(self, copy, when=None):
        self.started.append((copy, when))
        if when is None:
            copy.start()
        else:
            pl.when(when)(lambda: copy.start())

    def finish(self):
        for copy, when in self.started:
            if when is None:
                copy.wait_send()
            else:
                pl.when(when)(lambda copy=copy: copy.wait_send())


def whole(
    tokens_ref, gain_ref, grad_ref, wq_ref, wk_ref, wv_ref, out_ref,
    tok, gain, w, g, dout, qb, kv, kt, e_buf, dp_buf, b_buf, dr_buf, acc,
    back_out, back_near, back_far, grads, total, got_opp, got_x, got_za, got_zb,
    load_sem, sx, rx, szb, rzb, sza, rza, s_near, r_near, s_far, r_far,
    s_bn, r_bn, s_bf, r_bf, s1, r1, s2, r2, tza, uza, tzb, uzb,
):
    x, z = place()
    s = lax.axis_index("seq")
    blocks = lax.axis_size("seq")
    rows, width = tok.shape
    half = rows // 2
    a_width = A_TILES * 128
    a_cols = pl.ds(0, a_width)
    b_cols = pl.ds(a_width, width - a_width)
    xp, xm, xo = (x + 1) % NX, (x + 3) % NX, (x + 2) % NX
    zs = near_to_far(z)
    q_cols, k_cols = wq_ref.shape[1], wk_ref.shape[1]
    barrier, partners = greet_partners(x, z, s, blocks)
    loads = [
        pltpu.make_async_copy(tokens_ref, tok, load_sem.at[0]),
        pltpu.make_async_copy(gain_ref, gain, load_sem.at[1]),
        pltpu.make_async_copy(wq_ref, w.at[:, pl.ds(0, q_cols)], load_sem.at[2]),
        pltpu.make_async_copy(wk_ref, w.at[:, pl.ds(q_cols, k_cols)], load_sem.at[3]),
        pltpu.make_async_copy(wv_ref, w.at[:, pl.ds(q_cols + k_cols, k_cols)], load_sem.at[4]),
        pltpu.make_async_copy(grad_ref, dout, load_sem.at[5]),
    ]
    for load in loads:
        load.start()
    loads[0].wait()
    loads[1].wait()
    values = tok[...].astype(jnp.float32)
    inv_rms = lax.rsqrt(jnp.mean(values * values, axis=1, keepdims=True) + EPS)
    g[z, pl.ds(x * rows, rows), :] = (values * inv_rms * gain[...]).astype(jnp.bfloat16)
    pl.semaphore_wait(barrier, partners)
    sends = Sends()

    def part(zr, xr, h, cols):
        if h is None:
            return g.at[zr, pl.ds(pl.multiple_of(xr * rows, rows), rows), cols]
        return g.at[zr, pl.ds(pl.multiple_of(xr * rows + h * half, half), half), cols]

    def x_send(k, zr, xr, h, cols, to, direction, slot):
        piece = part(zr, xr, h, cols)
        p = 1 if k == NZ else 0
        sends.start(
            send_to(piece, piece, sx.at[direction, k, slot], rx.at[p, zr, xr, h], tp_of(to, z))
        )

    def x_wait(k, zr, xr, h, cols):
        piece = part(zr, xr, h, cols)
        p = 1 if k == NZ else 0
        send_to(piece, piece, sx.at[0, k, 0], rx.at[p, zr, xr, h], tp_of(xp, z)).wait_recv()

    def x_own(k, zr, cols, first):
        h_right, h_left = (0, 1) if first else (1, 0)
        slot = 0 if first else 1
        x_send(k, zr, x, h_right, cols, xp, 0, slot)
        x_send(k, zr, x, h_left, cols, xm, 1, slot)

    def x_forward(k, zr, cols):
        x_wait(k, zr, xm, 0, cols)
        x_send(k, zr, xm, 0, cols, xp, 0, 2)
        x_wait(k, zr, xp, 1, cols)
        x_send(k, zr, xp, 1, cols, xm, 1, 2)

    def x_rest(k, zr, cols):
        x_wait(k, zr, xm, 1, cols)
        x_wait(k, zr, xp, 0, cols)
        x_wait(k, zr, xo, 0, cols)
        x_wait(k, zr, xo, 1, cols)

    def z_piece(zr, is_a):
        return g.at[zr, :, a_cols] if is_a else part(zr, x, None, b_cols)

    def z_send(k, zr, is_a):
        piece = z_piece(zr, is_a)
        ss, rs = (sza, rza) if is_a else (szb, rzb)
        up = send_to(piece, piece, ss.at[0, k], rs.at[zr], tp_of(x, jnp.minimum(z + 1, NZ - 1)))
        down = send_to(piece, piece, ss.at[1, k], rs.at[zr], tp_of(x, jnp.maximum(z - 1, 0)))
        sends.start(up, (zr <= z) & (z < NZ - 1))
        sends.start(down, (zr >= z) & (z > 0))

    def z_wait(zr, is_a):
        piece = z_piece(zr, is_a)
        ss, rs = (sza, rza) if is_a else (szb, rzb)
        send_to(piece, piece, ss.at[0, 0], rs.at[zr], tp_of(xp, z)).wait_recv()

    def slab(first, count, zr):
        return kv.at[pl.ds(first, count), pl.ds(pl.multiple_of(zr * rows, rows), rows), :]

    def near_copy(k, zr):
        return send_along(
            slab(5, 4, zr), slab(1, 4, zr), s_near.at[k], r_near.at[k],
            jnp.minimum(s + 1, blocks - 1),
        )

    def far_copy(k, zr):
        return send_along(
            slab(8, 1, zr), slab(0, 1, zr), s_far.at[k], r_far.at[k],
            jnp.minimum(s + 2, blocks - 1),
        )

    def project(k):
        zr = zs[k]
        out = jnp.dot(g[zr], w[...], preferred_element_type=jnp.float32).astype(jnp.bfloat16)
        at = pl.ds(pl.multiple_of(zr * rows, rows), rows)
        for i in range(NX):
            kv[5 + i, at, :] = out[i * rows : (i + 1) * rows, q_cols:]
            qb[i, at, :] = out[i * rows : (i + 1) * rows, :q_cols]
        sends.start(near_copy(k, zr), s + 1 < blocks)
        sends.start(far_copy(k, zr), s + 2 < blocks)

    x_own(NZ, z, a_cols, True)
    x_own(NZ, z, a_cols, False)
    z_send(0, z, False)
    x_own(0, z, b_cols, True)
    x_forward(NZ, z, a_cols)
    x_own(0, z, b_cols, False)
    x_rest(NZ, z, a_cols)
    z_send(0, z, True)
    for load in loads[2:]:
        load.wait()
    acc[...] = jnp.zeros_like(acc)

    @pl.when(s == 0)
    def _():
        kv[0:5] = jnp.zeros_like(kv[0:5])

    @pl.when(s == 1)
    def _():
        kv[0] = jnp.zeros_like(kv[0])

    @pl.when(s == blocks - 1)
    def _():
        back_near[...] = jnp.zeros_like(back_near)

    @pl.when(s >= blocks - 2)
    def _():
        back_far[...] = jnp.zeros_like(back_far)

    for k in range(1, NZ):
        zr, before = zs[k], zs[k - 1]
        x_forward(k - 1, before, b_cols)
        z_wait(zr, False)
        z_send(k, zr, False)
        x_own(k, zr, b_cols, True)
        x_own(k, zr, b_cols, False)
        z_wait(zr, True)
        z_send(k, zr, True)
        x_rest(k - 1, before, b_cols)
        project(k - 1)
    x_forward(NZ - 1, zs[-1], b_cols)
    x_rest(NZ - 1, zs[-1], b_cols)
    project(NZ - 1)

    hd = HEAD_SIZE
    last = (((1,), (1,)), ((), ()))

    def two_heads(ref, qt):
        return jnp.concatenate([ref[qt, :, 0:hd], ref[qt, :, hd : 2 * hd]], axis=0)

    row_at = lax.broadcasted_iota(jnp.int32, (hd, 2 * hd), 0)
    col_at = lax.broadcasted_iota(jnp.int32, (hd, 2 * hd), 1) % hd

    def scores(qt, c, q2, do2):
        j = qt + c
        raw = lax.dot_general(kv[j, :, 0:hd], q2, last, preferred_element_type=jnp.float32)
        bent = jnp.tanh(raw * (SCALE / CAP))
        expo = jnp.exp(CAP * bent)
        if c == 0:
            expo = jnp.where(row_at > col_at, expo, 0.0)
        if c == 5:
            expo = jnp.where(row_at <= col_at, expo, 0.0)
        if j < 5:
            expo = expo * jnp.where(s >= (1 if j > 0 else 2), 1.0, 0.0)
        d_probs = lax.dot_general(
            kv[j, :, hd : 2 * hd], do2, last, preferred_element_type=jnp.float32
        )
        e_buf[qt, c] = expo
        dp_buf[qt, c] = d_probs
        b_buf[qt, c] = bent
        shape = (hd // 8, 8, 2 * hd)
        return (
            jnp.sum(expo.reshape(shape), axis=0),
            jnp.sum((expo * d_probs).reshape(shape), axis=0),
        )

    def transpose_keys(j):
        kt[:, pl.ds(j * hd, hd)] = kv[j, :, 0:hd].astype(jnp.float32).T.astype(jnp.bfloat16)

    sums = []
    for qt in range(NX):
        q2, do2 = two_heads(qb, qt), two_heads(dout, qt)
        parts = [scores(qt, c, q2, do2) for c in range(5 - qt, 6)]
        sums.append((sum(p[0] for p in parts), sum(p[1] for p in parts)))
    for j in range(5, 9):
        transpose_keys(j)

    @pl.when(s > 0)
    def _():
        for k in range(NZ):
            near_copy(k, zs[k]).wait_recv()

    @pl.when(s > 1)
    def _():
        for k in range(NZ):
            far_copy(k, zs[k]).wait_recv()

    for j in range(5):
        transpose_keys(j)

    gathering, sends = sends, Sends()

    def give_back(j):
        back_out[j] = acc[j].astype(jnp.bfloat16)
        if j == 0:
            far = send_along(
                back_out.at[0], back_far, s_bf.at[0], r_bf.at[0], jnp.maximum(s - 2, 0)
            )
            sends.start(far, s > 1)
        else:
            near = send_along(
                back_out.at[j], back_near.at[j - 1], s_bn.at[j - 1], r_bn.at[j - 1],
                jnp.maximum(s - 1, 0),
            )
            sends.start(near, s > 0)

    for qt in range(NX):
        q2, do2 = two_heads(qb, qt), two_heads(dout, qt)
        parts = [scores(qt, c, q2, do2) for c in range(0, 5 - qt)]
        norm = jnp.sum(sums[qt][0] + sum(p[0] for p in parts), axis=0, keepdims=True)
        inner = jnp.sum(sums[qt][1] + sum(p[1] for p in parts), axis=0, keepdims=True)
        inverse = 1.0 / norm
        delta = inner * inverse
        for c in range(6):
            probs = e_buf[qt, c] * inverse
            bent = b_buf[qt, c]
            d_raw = (
                probs * (dp_buf[qt, c] - delta) * (1.0 - bent * bent) * SCALE
            ).astype(jnp.bfloat16)
            dr_buf[pl.ds(c * hd, hd), :] = d_raw
            acc[qt + c, :, 0:hd] += jnp.dot(d_raw, q2, preferred_element_type=jnp.float32)
            acc[qt + c, :, hd : 2 * hd] += jnp.dot(
                probs.astype(jnp.bfloat16), do2, preferred_element_type=jnp.float32
            )
        d_query = jnp.dot(
            kt[:, pl.ds(qt * hd, 6 * hd)], dr_buf[...], preferred_element_type=jnp.float32
        )
        grads[qt, :, 0:hd] = d_query[:, 0:hd].T.astype(jnp.bfloat16)
        grads[qt, :, hd : 2 * hd] = d_query[:, hd : 2 * hd].T.astype(jnp.bfloat16)
        give_back(qt)
    give_back(4)

    @pl.when(s < blocks - 2)
    def _():
        send_along(back_out.at[0], back_far, s_bf.at[0], r_bf.at[0], s).wait_recv()

    @pl.when(s < blocks - 1)
    def _():
        for i in range(NX):
            send_along(
                back_out.at[i + 1], back_near.at[i], s_bn.at[i], r_bn.at[i], s
            ).wait_recv()

    for i in range(NX):
        own = acc[5 + i] + back_near[i].astype(jnp.float32)
        if i == NX - 1:
            own = own + back_far[...].astype(jnp.float32)
        grads[i, :, q_cols:] = own.astype(jnp.bfloat16)

    gathering.finish()
    zs = zs[::-1]
    p = g
    tile = 512

    def row_ds(xr, h=None):
        if h is None:
            return pl.ds(pl.multiple_of(xr * rows, rows), rows)
        return pl.ds(pl.multiple_of(xr * rows + h * half, half), half)

    def compute(zr):
        lhs = grads[:, pl.ds(pl.multiple_of(zr * rows, rows), rows), :].reshape(NX * rows, -1)

        @pl.loop(0, width // tile)
        def _(j):
            at = pl.ds(pl.multiple_of(j * tile, tile), tile)
            p[zr, :, at] = lax.dot_general(
                lhs, w[at, :], (((1,), (1,)), ((), ())), preferred_element_type=jnp.float32
            ).astype(jnp.bfloat16)

    def far_exists(zr):
        return ((zr < z) & (z < NZ - 1)) | ((zr > z) & (z > 0))

    def way(zr):
        return jnp.where(zr > z, 1, 0)

    def nearer(zr):
        return tp_of(x, jnp.where(zr > z, z + 1, z - 1))

    def step1(k, zr, cols):
        for direction, to in ((0, xm), (1, xp)):
            sends.start(
                send_to(
                    p.at[zr, row_ds(xo, direction), cols],
                    got_opp.at[direction, zr, :, cols],
                    s1.at[direction, k],
                    r1.at[direction, k],
                    tp_of(to, z),
                )
            )

    def step2(k, zr, cols):
        for direction, to in ((0, xm), (1, xp)):
            land = got_opp.at[direction, zr, :, cols]
            send_to(land, land, s1.at[direction, k], r1.at[direction, k], tp_of(to, z)).wait_recv()
            at = row_ds(to, direction)
            p[zr, at, cols] = (
                p[zr, at, cols].astype(jnp.float32)
                + got_opp[direction, zr, :, cols].astype(jnp.float32)
            ).astype(jnp.bfloat16)
            sends.start(
                send_to(
                    p.at[zr, row_ds(to), cols],
                    got_x.at[direction, zr, :, cols],
                    s2.at[direction, k],
                    r2.at[direction, k],
                    tp_of(to, z),
                )
            )

    def x_sum(k, zr, cols):
        for direction, to in ((0, xm), (1, xp)):
            land = got_x.at[direction, zr, :, cols]
            send_to(land, land, s2.at[direction, k], r2.at[direction, k], tp_of(to, z)).wait_recv()
        return (
            p[zr, row_ds(x), cols].astype(jnp.float32)
            + got_x[0, zr, :, cols].astype(jnp.float32)
            + got_x[1, zr, :, cols].astype(jnp.float32)
        )

    def z_wait_b(d, zr):
        land = got_zb.at[d, zr]
        send_to(land, land, tzb.at[0], uzb.at[d, zr], tp_of(xp, z)).wait_recv()

    def z_wait_a(d, zr):
        land = got_za.at[d, zr]
        send_to(land, land, tza.at[0], uza.at[d, zr], tp_of(xp, z)).wait_recv()

    def step3(k, zr, far):
        copy = send_to(
            p.at[zr, row_ds(x), b_cols], got_zb.at[way(zr), zr], tzb.at[k],
            uzb.at[way(zr), zr], nearer(zr),
        )

        def run():
            value = x_sum(k, zr, b_cols)
            if far:
                z_wait_b(way(zr), zr)
                value = value + got_zb[way(zr), zr].astype(jnp.float32)
            p[zr, row_ds(x), b_cols] = value.astype(jnp.bfloat16)
            copy.start()

        if far:
            pl.when(far_exists(zr))(run)
            sends.started.append((copy, None))
        else:
            pl.when(jnp.logical_not(far_exists(zr)))(run)

    def line_a(k, zr, far):
        copy = send_to(
            p.at[zr, :, a_cols], got_za.at[way(zr), zr], tza.at[k],
            uza.at[way(zr), zr], nearer(zr),
        )

        def run():
            if far:
                z_wait_a(way(zr), zr)
                p[zr, :, a_cols] = (
                    p[zr, :, a_cols].astype(jnp.float32)
                    + got_za[way(zr), zr].astype(jnp.float32)
                ).astype(jnp.bfloat16)
            copy.start()

        if far:
            pl.when(far_exists(zr))(run)
            sends.started.append((copy, None))
        else:
            pl.when(jnp.logical_not(far_exists(zr)))(run)

    compute(zs[0])
    step1(0, zs[0], b_cols)
    line_a(0, zs[0], False)
    compute(zs[1])
    step1(1, zs[1], b_cols)
    line_a(1, zs[1], False)
    step2(0, zs[0], b_cols)
    line_a(0, zs[0], True)
    compute(zs[2])
    step1(2, zs[2], b_cols)
    line_a(2, zs[2], False)
    step2(1, zs[1], b_cols)
    line_a(1, zs[1], True)
    step3(0, zs[0], False)
    compute(z)
    step1(3, z, b_cols)
    step2(2, zs[2], b_cols)
    line_a(2, zs[2], True)
    step3(1, zs[1], False)
    step3(0, zs[0], True)
    step2(3, z, b_cols)
    step3(2, zs[2], False)

    for d, there in ((0, z < NZ - 1), (1, z > 0)):

        @pl.when(there)
        def _(d=d):
            z_wait_a(d, z)
            p[z, :, a_cols] = (
                p[z, :, a_cols].astype(jnp.float32) + got_za[d, z].astype(jnp.float32)
            ).astype(jnp.bfloat16)

    step1(4, z, a_cols)
    step3(1, zs[1], True)
    step2(4, z, a_cols)
    step3(2, zs[2], True)
    total[:, b_cols] = x_sum(3, z, b_cols)
    for d, there in ((0, z < NZ - 1), (1, z > 0)):

        @pl.when(there)
        def _(d=d):
            z_wait_b(d, z)
            total[:, b_cols] = total[:, b_cols] + got_zb[d, z].astype(jnp.float32)

    total[:, a_cols] = x_sum(4, z, a_cols)
    values = tok[...].astype(jnp.float32)
    inv_rms = lax.rsqrt(jnp.mean(values * values, axis=1, keepdims=True) + EPS)
    upper = total[...] * gain[...]
    xhat = values * inv_rms
    out_ref[...] = (
        inv_rms * (upper - xhat * jnp.mean(upper * xhat, axis=1, keepdims=True))
    ).astype(jnp.bfloat16)
    sends.finish()


def on_device(tokens, norm_gain, query_weight, key_matrix, value_matrix, output_grad):
    rows, width = tokens.shape
    q_cols, k_cols = query_weight.shape[1], key_matrix.shape[1]
    cols = q_cols + 2 * k_cols
    a_width = A_TILES * 128
    hd = HEAD_SIZE
    any_space = pl.BlockSpec(memory_space=pl.ANY)
    dma = pltpu.SemaphoreType.DMA
    low, full = jnp.bfloat16, jnp.float32

    def vmem(kind, *shape):
        return pltpu.VMEM(shape, kind)

    return pl.pallas_call(
        whole,
        out_shape=jax.ShapeDtypeStruct((rows, width), low),
        in_specs=[any_space] * 6,
        out_specs=pl.BlockSpec(memory_space=pltpu.VMEM),
        scratch_shapes=[
            vmem(low, rows, width),
            vmem(full, 1, width),
            vmem(low, width, cols),
            vmem(low, NZ, NX * rows, width),
            vmem(low, NX, hd, q_cols),
            vmem(low, NX, hd, q_cols),
            vmem(low, 9, hd, 2 * k_cols),
            vmem(low, hd, 9 * hd),
            vmem(full, NX, 6, hd, 2 * hd),
            vmem(full, NX, 6, hd, 2 * hd),
            vmem(full, NX, 6, hd, 2 * hd),
            vmem(low, 6 * hd, 2 * hd),
            vmem(full, 9, hd, 2 * k_cols),
            vmem(low, 5, hd, 2 * k_cols),
            vmem(low, NX, hd, 2 * k_cols),
            vmem(low, hd, 2 * k_cols),
            vmem(low, NX, hd, cols),
            vmem(full, rows, width),
            vmem(low, 2, NZ, rows // 2, width),
            vmem(low, 2, NZ, rows, width),
            vmem(low, 2, NZ, NX * rows, a_width),
            vmem(low, 2, NZ, rows, width - a_width),
            dma((6,)),
            dma((2, NZ + 1, 3)),
            dma((2, NZ, NX, 2)),
            dma((2, NZ)),
            dma((NZ,)),
            dma((2, NZ)),
            dma((NZ,)),
            dma((NZ,)),
            dma((NZ,)),
            dma((NZ,)),
            dma((NZ,)),
            dma((NX,)),
            dma((NX,)),
            dma((1,)),
            dma((1,)),
            dma((2, NZ + 1)),
            dma((2, NZ + 1)),
            dma((2, NZ + 1)),
            dma((2, NZ + 1)),
            dma((NZ,)),
            dma((2, NZ)),
            dma((NZ,)),
            dma((2, NZ)),
        ],
        compiler_params=pltpu.CompilerParams(
            collective_id=0, has_side_effects=True, vmem_limit_bytes=62 * 1024 * 1024
        ),
    )(
        tokens,
        norm_gain.reshape(1, -1),
        output_grad.reshape(NX, hd, q_cols),
        query_weight,
        key_matrix,
        value_matrix,
    )


def solution(mesh):
    tp, both = "tp", ("seq", "tp")
    in_specs = (P(both, None), P(), P(None, tp), P(None, tp), P(None, tp), P("seq", tp))
    return jax.shard_map(
        on_device, mesh=mesh, in_specs=in_specs, out_specs=P(both, None), check_vma=False
    )
```

time: 163 us -> 118 us (0.72)
  the two profiles are of different devices: /device:TPU:24 before, /device:TPU:1 now
where the time goes in v2:
time: 118 us; the launch traced here: 117 us
  Pallas kernels  114 us (97%)
  local copies, waits for them, and re-layouts  3.04 us (3%)
    pallas_call x1, Pallas kernels, on_device(): pl.pallas_call(whole, out_shape=jax.ShapeDtypeStruct((rows, width), low),...  114 us

profile of v2, /device:TPU:1, one launch (start us, length us, event | category | flops | bytes accessed | tf_op | source)
XLA Modules:
  0.0 117.4 jit_solution(7999547053604263745)
XLA Ops:
  0.0 1.3 %reshape.6.gain_ref = f32[1,4608]{1,0:T(1,128)} reshape(f32[4608]{0:T(1024)} %param.7) | data formatting | bytes 36864 | tf_op jit(solution)/shard_map/reshape | solution.py:611
  1.3 114.4 %shard_map.64 = bf16[32,4608]{1,0:T(8,128)(2,1)} custom-call(bf16[32,4608]{1,0:T(8,128)(2,1)} %tokens_ref.1, f32[1,4608]{1,0:T(1,128)} %reshape.6.gain_ref, bf16[4,128,256]{2,1,0:T(8,128)(2,1)} %bitcast.1, bf16[4608,256]{1,0:T(8,128)(2,1)} %wq_ref.1, bf16[4608,128]{1,0:T(8,128)(2,1)} %wk_ref.1, bf16[4608,128]{1,0:T(8,128)(2,1)} %wv_ref.1), custom_call_target="tpu_custom_call" | custom-call | tf_op jit(solution)/shard_map/pallas_call | solution.py:554
  115.8 1.7 %copy.8 = bf16[32,4608]{1,0:T(8,128)(2,1)} copy(bf16[32,4608]{1,0:T(8,128)(2,1)} %shard_map.64) | data formatting | bytes 589824

commit v3 on v2

--- a/solution.py
+++ b/solution.py
@@ -14,6 +14,8 @@
 NX = 4
 NZ = 4
 A_TILES = 8
+TURN = 512
+TURNS = 9
 
 
 def place():
@@ -95,7 +97,7 @@
 
 def whole(
     tokens_ref, gain_ref, grad_ref, wq_ref, wk_ref, wv_ref, out_ref,
-    tok, gain, w, g, dout, qb, kv, kt, e_buf, dp_buf, b_buf, dr_buf, acc,
+    tok, gain, w, wt, g, dout, qb, kv, kt, e_buf, dp_buf, b_buf, dr_buf, acc,
     back_out, back_near, back_far, grads, total, got_opp, got_x, got_za, got_zb,
     load_sem, sx, rx, szb, rzb, sza, rza, s_near, r_near, s_far, r_far,
     s_bn, r_bn, s_bf, r_bf, s1, r1, s2, r2, tza, uza, tzb, uzb,
@@ -159,27 +161,40 @@
         x_wait(k, zr, xp, 1, cols)
         x_send(k, zr, xp, 1, cols, xm, 1, 2)
 
-    def x_rest(k, zr, cols):
+    def x_rest_near(k, zr, cols):
         x_wait(k, zr, xm, 1, cols)
         x_wait(k, zr, xp, 0, cols)
+
+    def x_rest_opposite(k, zr, cols):
         x_wait(k, zr, xo, 0, cols)
         x_wait(k, zr, xo, 1, cols)
 
-    def z_piece(zr, is_a):
-        return g.at[zr, :, a_cols] if is_a else part(zr, x, None, b_cols)
-
-    def z_send(k, zr, is_a):
-        piece = z_piece(zr, is_a)
-        ss, rs = (sza, rza) if is_a else (szb, rzb)
-        up = send_to(piece, piece, ss.at[0, k], rs.at[zr], tp_of(x, jnp.minimum(z + 1, NZ - 1)))
-        down = send_to(piece, piece, ss.at[1, k], rs.at[zr], tp_of(x, jnp.maximum(z - 1, 0)))
-        sends.start(up, (zr <= z) & (z < NZ - 1))
-        sends.start(down, (zr >= z) & (z > 0))
-
-    def z_wait(zr, is_a):
-        piece = z_piece(zr, is_a)
-        ss, rs = (sza, rza) if is_a else (szb, rzb)
-        send_to(piece, piece, ss.at[0, 0], rs.at[zr], tp_of(xp, z)).wait_recv()
+    def x_rest(k, zr, cols):
+        x_rest_near(k, zr, cols)
+        x_rest_opposite(k, zr, cols)
+
+    def z_send_b(k, zr, way, to):
+        piece = part(zr, x, None, b_cols)
+        sends.start(send_to(piece, piece, szb.at[way, k], rzb.at[zr], tp_of(x, to)))
+
+    def z_send_a(k, zr, xr, way, to):
+        piece = part(zr, xr, None, a_cols)
+        sends.start(
+            send_to(piece, piece, sza.at[way, k, xr], rza.at[zr, xr], tp_of(x, to))
+        )
+
+    def z_wait_b(k):
+        piece = part(zs[k], x, None, b_cols)
+        send_to(piece, piece, szb.at[0, 0], rzb.at[zs[k]], tp_of(xp, z)).wait_recv()
+
+    def z_wait_a(k):
+        for i in range(NX):
+            piece = part(zs[k], i, None, a_cols)
+            send_to(piece, piece, sza.at[0, 0, i], rza.at[zs[k], i], tp_of(xp, z)).wait_recv()
+
+    def turn(c):
+        at = pl.ds(c * TURN, TURN)
+        wt[:, at] = w[at, :].T
 
     def slab(first, count, zr):
         return kv.at[pl.ds(first, count), pl.ds(pl.multiple_of(zr * rows, rows), rows), :]
@@ -203,51 +218,129 @@
         for i in range(NX):
             kv[5 + i, at, :] = out[i * rows : (i + 1) * rows, q_cols:]
             qb[i, at, :] = out[i * rows : (i + 1) * rows, :q_cols]
-        sends.start(near_copy(k, zr), s + 1 < blocks)
-        sends.start(far_copy(k, zr), s + 2 < blocks)
-
-    x_own(NZ, z, a_cols, True)
-    x_own(NZ, z, a_cols, False)
-    z_send(0, z, False)
-    x_own(0, z, b_cols, True)
-    x_forward(NZ, z, a_cols)
-    x_own(0, z, b_cols, False)
-    x_rest(NZ, z, a_cols)
-    z_send(0, z, True)
-    for load in loads[2:]:
-        load.wait()
-    acc[...] = jnp.zeros_like(acc)
-
-    @pl.when(s == 0)
-    def _():
-        kv[0:5] = jnp.zeros_like(kv[0:5])
-
-    @pl.when(s == 1)
-    def _():
-        kv[0] = jnp.zeros_like(kv[0])
-
-    @pl.when(s == blocks - 1)
-    def _():
-        back_near[...] = jnp.zeros_like(back_near)
-
-    @pl.when(s >= blocks - 2)
-    def _():
-        back_far[...] = jnp.zeros_like(back_far)
-
-    for k in range(1, NZ):
-        zr, before = zs[k], zs[k - 1]
-        x_forward(k - 1, before, b_cols)
-        z_wait(zr, False)
-        z_send(k, zr, False)
-        x_own(k, zr, b_cols, True)
-        x_own(k, zr, b_cols, False)
-        z_wait(zr, True)
-        z_send(k, zr, True)
-        x_rest(k - 1, before, b_cols)
-        project(k - 1)
-    x_forward(NZ - 1, zs[-1], b_cols)
-    x_rest(NZ - 1, zs[-1], b_cols)
-    project(NZ - 1)
+        pl.when(s + 1 < blocks)(lambda: near_copy(k, zr).start())
+        pl.when(s + 2 < blocks)(lambda: far_copy(k, zr).start())
+
+    is_edge = (z == 0) | (z == NZ - 1)
+
+    def start_gather(neighbours):
+        x_own(NZ, z, a_cols, True)
+        x_own(NZ, z, a_cols, False)
+        for way, to in neighbours:
+            z_send_b(0, z, way, to)
+        x_own(0, z, b_cols, True)
+        x_forward(NZ, z, a_cols)
+        x_own(0, z, b_cols, False)
+        way, to = neighbours[0]
+        x_rest_near(NZ, z, a_cols)
+        for i in (x, xm, xp):
+            z_send_a(0, z, i, way, to)
+        for load in loads[2:]:
+            load.wait()
+        clear_edges()
+        turn(0)
+        x_rest_opposite(NZ, z, a_cols)
+        z_send_a(0, z, xo, way, to)
+        x_forward(0, z, b_cols)
+
+    def clear_edges():
+        @pl.when(s == 0)
+        def _():
+            kv[0:5] = jnp.zeros_like(kv[0:5])
+
+        @pl.when(s == 1)
+        def _():
+            kv[0] = jnp.zeros_like(kv[0])
+
+        @pl.when(s == blocks - 1)
+        def _():
+            back_near[...] = jnp.zeros_like(back_near)
+
+        @pl.when(s >= blocks - 2)
+        def _():
+            back_far[...] = jnp.zeros_like(back_far)
+
+    @pl.when(is_edge)
+    def _():
+        start_gather([(0, jnp.where(z == 0, 1, NZ - 2))])
+        z_wait_b(1)
+        x_own(1, zs[1], b_cols, True)
+        x_own(1, zs[1], b_cols, False)
+        for c in range(1, 5):
+            turn(c)
+        x_rest(0, z, b_cols)
+        project(0)
+        x_forward(1, zs[1], b_cols)
+        turn(5)
+        z_wait_b(2)
+        x_own(2, zs[2], b_cols, True)
+        x_own(2, zs[2], b_cols, False)
+        z_wait_a(1)
+        x_rest(1, zs[1], b_cols)
+        project(1)
+        x_forward(2, zs[2], b_cols)
+        z_wait_b(3)
+        x_own(3, zs[3], b_cols, True)
+        x_own(3, zs[3], b_cols, False)
+        for c in range(6, TURNS):
+            turn(c)
+        z_wait_a(2)
+        x_rest(2, zs[2], b_cols)
+        project(2)
+        x_forward(3, zs[3], b_cols)
+        z_wait_a(3)
+        x_rest(3, zs[3], b_cols)
+        project(3)
+        sends.finish()
+
+    sends = Sends()
+
+    @pl.when(jnp.logical_not(is_edge))
+    def _():
+        outer = jnp.where(z == 1, 0, NZ - 1)
+        inner = NZ - 1 - z
+        start_gather([(0, outer), (1, inner)])
+        z_wait_b(1)
+        z_send_b(1, zs[1], 1, inner)
+        for i in (x, xm, xp, xo):
+            z_send_a(0, z, i, 1, inner)
+        x_own(1, zs[1], b_cols, True)
+        x_own(1, zs[1], b_cols, False)
+        z_wait_b(2)
+        z_send_b(2, zs[2], 0, outer)
+        x_own(2, zs[2], b_cols, True)
+        x_own(2, zs[2], b_cols, False)
+        for c in range(1, 4):
+            turn(c)
+        x_rest(0, z, b_cols)
+        project(0)
+        z_wait_a(1)
+        for i in range(NX):
+            z_send_a(1, zs[1], i, 1, inner)
+        z_wait_b(3)
+        z_send_b(3, zs[3], 0, outer)
+        x_forward(1, zs[1], b_cols)
+        x_own(3, zs[3], b_cols, True)
+        x_own(3, zs[3], b_cols, False)
+        for c in range(4, 7):
+            turn(c)
+        x_forward(2, zs[2], b_cols)
+        z_wait_a(2)
+        for i in range(NX):
+            z_send_a(2, zs[2], i, 0, outer)
+        for c in range(7, TURNS):
+            turn(c)
+        x_rest(1, zs[1], b_cols)
+        project(1)
+        z_wait_a(3)
+        for i in range(NX):
+            z_send_a(3, zs[3], i, 0, outer)
+        x_forward(3, zs[3], b_cols)
+        x_rest(2, zs[2], b_cols)
+        project(2)
+        x_rest(3, zs[3], b_cols)
+        project(3)
+        sends.finish()
 
     hd = HEAD_SIZE
     last = (((1,), (1,)), ((), ()))
@@ -305,47 +398,60 @@
     for j in range(5):
         transpose_keys(j)
 
-    gathering, sends = sends, Sends()
-
-    def give_back(j):
-        back_out[j] = acc[j].astype(jnp.bfloat16)
-        if j == 0:
-            far = send_along(
-                back_out.at[0], back_far, s_bf.at[0], r_bf.at[0], jnp.maximum(s - 2, 0)
-            )
-            sends.start(far, s > 1)
-        else:
-            near = send_along(
-                back_out.at[j], back_near.at[j - 1], s_bn.at[j - 1], r_bn.at[j - 1],
-                jnp.maximum(s - 1, 0),
-            )
-            sends.start(near, s > 0)
-
+    rest = []
     for qt in range(NX):
         q2, do2 = two_heads(qb, qt), two_heads(dout, qt)
         parts = [scores(qt, c, q2, do2) for c in range(0, 5 - qt)]
         norm = jnp.sum(sums[qt][0] + sum(p[0] for p in parts), axis=0, keepdims=True)
         inner = jnp.sum(sums[qt][1] + sum(p[1] for p in parts), axis=0, keepdims=True)
         inverse = 1.0 / norm
-        delta = inner * inverse
-        for c in range(6):
+        rest.append((inverse, inner * inverse))
+
+    def tile_grads(j):
+        d_key = d_value = 0.0
+        for qt in range(max(0, j - 5), min(NX, j + 1)):
+            c = j - qt
+            inverse, delta = rest[qt]
             probs = e_buf[qt, c] * inverse
             bent = b_buf[qt, c]
             d_raw = (
                 probs * (dp_buf[qt, c] - delta) * (1.0 - bent * bent) * SCALE
             ).astype(jnp.bfloat16)
-            dr_buf[pl.ds(c * hd, hd), :] = d_raw
-            acc[qt + c, :, 0:hd] += jnp.dot(d_raw, q2, preferred_element_type=jnp.float32)
-            acc[qt + c, :, hd : 2 * hd] += jnp.dot(
-                probs.astype(jnp.bfloat16), do2, preferred_element_type=jnp.float32
+            dr_buf[qt, pl.ds(c * hd, hd), :] = d_raw
+            d_key += jnp.dot(d_raw, two_heads(qb, qt), preferred_element_type=jnp.float32)
+            d_value += jnp.dot(
+                probs.astype(jnp.bfloat16), two_heads(dout, qt), preferred_element_type=jnp.float32
             )
+        return d_key, d_value
+
+    far_back = send_along(
+        back_out.at[0], back_far, s_bf.at[0], r_bf.at[0], jnp.maximum(s - 2, 0)
+    )
+    near_back = [
+        send_along(
+            back_out.at[j], back_near.at[j - 1], s_bn.at[j - 1], r_bn.at[j - 1],
+            jnp.maximum(s - 1, 0),
+        )
+        for j in range(1, 5)
+    ]
+    for j in range(5):
+        d_key, d_value = tile_grads(j)
+        back_out[j, :, 0:hd] = d_key.astype(jnp.bfloat16)
+        back_out[j, :, hd : 2 * hd] = d_value.astype(jnp.bfloat16)
+        if j == 0:
+            pl.when(s > 1)(lambda: far_back.start())
+        else:
+            pl.when(s > 0)(lambda j=j: near_back[j - 1].start())
+    for j in range(5, 9):
+        d_key, d_value = tile_grads(j)
+        acc[j - 5, :, 0:hd] = d_key
+        acc[j - 5, :, hd : 2 * hd] = d_value
+    for qt in range(NX):
         d_query = jnp.dot(
-            kt[:, pl.ds(qt * hd, 6 * hd)], dr_buf[...], preferred_element_type=jnp.float32
+            kt[:, pl.ds(qt * hd, 6 * hd)], dr_buf[qt], preferred_element_type=jnp.float32
         )
         grads[qt, :, 0:hd] = d_query[:, 0:hd].T.astype(jnp.bfloat16)
         grads[qt, :, hd : 2 * hd] = d_query[:, hd : 2 * hd].T.astype(jnp.bfloat16)
-        give_back(qt)
-    give_back(4)
 
     @pl.when(s < blocks - 2)
     def _():
@@ -359,12 +465,11 @@
             ).wait_recv()
 
     for i in range(NX):
-        own = acc[5 + i] + back_near[i].astype(jnp.float32)
+        own = acc[i] + back_near[i].astype(jnp.float32)
         if i == NX - 1:
             own = own + back_far[...].astype(jnp.float32)
         grads[i, :, q_cols:] = own.astype(jnp.bfloat16)
 
-    gathering.finish()
     zs = zs[::-1]
     p = g
     tile = 512
@@ -380,12 +485,9 @@
         @pl.loop(0, width // tile)
         def _(j):
             at = pl.ds(pl.multiple_of(j * tile, tile), tile)
-            p[zr, :, at] = lax.dot_general(
-                lhs, w[at, :], (((1,), (1,)), ((), ())), preferred_element_type=jnp.float32
+            p[zr, :, at] = jnp.dot(
+                lhs, wt[:, at], preferred_element_type=jnp.float32
             ).astype(jnp.bfloat16)
-
-    def far_exists(zr):
-        return ((zr < z) & (z < NZ - 1)) | ((zr > z) & (z > 0))
 
     def way(zr):
         return jnp.where(zr > z, 1, 0)
@@ -434,108 +536,134 @@
             + got_x[1, zr, :, cols].astype(jnp.float32)
         )
 
-    def z_wait_b(d, zr):
+    def line_wait_b(d, zr):
         land = got_zb.at[d, zr]
         send_to(land, land, tzb.at[0], uzb.at[d, zr], tp_of(xp, z)).wait_recv()
 
-    def z_wait_a(d, zr):
+    def line_wait_a(d, zr):
         land = got_za.at[d, zr]
         send_to(land, land, tza.at[0], uza.at[d, zr], tp_of(xp, z)).wait_recv()
 
-    def step3(k, zr, far):
-        copy = send_to(
-            p.at[zr, row_ds(x), b_cols], got_zb.at[way(zr), zr], tzb.at[k],
-            uzb.at[way(zr), zr], nearer(zr),
-        )
-
-        def run():
-            value = x_sum(k, zr, b_cols)
-            if far:
-                z_wait_b(way(zr), zr)
-                value = value + got_zb[way(zr), zr].astype(jnp.float32)
-            p[zr, row_ds(x), b_cols] = value.astype(jnp.bfloat16)
-            copy.start()
-
+    def step3(k, far):
+        zr = zs[k]
+        value = x_sum(k, zr, b_cols)
         if far:
-            pl.when(far_exists(zr))(run)
-            sends.started.append((copy, None))
-        else:
-            pl.when(jnp.logical_not(far_exists(zr)))(run)
-
-    def line_a(k, zr, far):
-        copy = send_to(
-            p.at[zr, :, a_cols], got_za.at[way(zr), zr], tza.at[k],
-            uza.at[way(zr), zr], nearer(zr),
-        )
-
-        def run():
-            if far:
-                z_wait_a(way(zr), zr)
-                p[zr, :, a_cols] = (
-                    p[zr, :, a_cols].astype(jnp.float32)
-                    + got_za[way(zr), zr].astype(jnp.float32)
-                ).astype(jnp.bfloat16)
-            copy.start()
-
+            line_wait_b(way(zr), zr)
+            value = value + got_zb[way(zr), zr].astype(jnp.float32)
+        p[zr, row_ds(x), b_cols] = value.astype(jnp.bfloat16)
+        sends.start(
+            send_to(
+                p.at[zr, row_ds(x), b_cols], got_zb.at[way(zr), zr], tzb.at[k],
+                uzb.at[way(zr), zr], nearer(zr),
+            )
+        )
+
+    def add_a(d, zr):
+        line_wait_a(d, zr)
+        p[zr, :, a_cols] = (
+            p[zr, :, a_cols].astype(jnp.float32) + got_za[d, zr].astype(jnp.float32)
+        ).astype(jnp.bfloat16)
+
+    def line_a(k, far):
+        zr = zs[k]
         if far:
-            pl.when(far_exists(zr))(run)
-            sends.started.append((copy, None))
-        else:
-            pl.when(jnp.logical_not(far_exists(zr)))(run)
-
-    compute(zs[0])
-    step1(0, zs[0], b_cols)
-    line_a(0, zs[0], False)
-    compute(zs[1])
-    step1(1, zs[1], b_cols)
-    line_a(1, zs[1], False)
-    step2(0, zs[0], b_cols)
-    line_a(0, zs[0], True)
-    compute(zs[2])
-    step1(2, zs[2], b_cols)
-    line_a(2, zs[2], False)
-    step2(1, zs[1], b_cols)
-    line_a(1, zs[1], True)
-    step3(0, zs[0], False)
-    compute(z)
-    step1(3, z, b_cols)
-    step2(2, zs[2], b_cols)
-    line_a(2, zs[2], True)
-    step3(1, zs[1], False)
-    step3(0, zs[0], True)
-    step2(3, z, b_cols)
-    step3(2, zs[2], False)
-
-    for d, there in ((0, z < NZ - 1), (1, z > 0)):
-
-        @pl.when(there)
-        def _(d=d):
-            z_wait_a(d, z)
-            p[z, :, a_cols] = (
-                p[z, :, a_cols].astype(jnp.float32) + got_za[d, z].astype(jnp.float32)
-            ).astype(jnp.bfloat16)
-
-    step1(4, z, a_cols)
-    step3(1, zs[1], True)
-    step2(4, z, a_cols)
-    step3(2, zs[2], True)
-    total[:, b_cols] = x_sum(3, z, b_cols)
-    for d, there in ((0, z < NZ - 1), (1, z > 0)):
-
-        @pl.when(there)
-        def _(d=d):
-            z_wait_b(d, z)
+            add_a(way(zr), zr)
+        sends.start(
+            send_to(
+                p.at[zr, :, a_cols], got_za.at[way(zr), zr], tza.at[k],
+                uza.at[way(zr), zr], nearer(zr),
+            )
+        )
+
+    def finish(sources):
+        total[:, b_cols] = x_sum(3, z, b_cols)
+        for d in sources:
+            line_wait_b(d, z)
             total[:, b_cols] = total[:, b_cols] + got_zb[d, z].astype(jnp.float32)
-
-    total[:, a_cols] = x_sum(4, z, a_cols)
-    values = tok[...].astype(jnp.float32)
-    inv_rms = lax.rsqrt(jnp.mean(values * values, axis=1, keepdims=True) + EPS)
-    upper = total[...] * gain[...]
-    xhat = values * inv_rms
-    out_ref[...] = (
-        inv_rms * (upper - xhat * jnp.mean(upper * xhat, axis=1, keepdims=True))
-    ).astype(jnp.bfloat16)
-    sends.finish()
+        total[:, a_cols] = x_sum(4, z, a_cols)
+        values = tok[...].astype(jnp.float32)
+        inv_rms = lax.rsqrt(jnp.mean(values * values, axis=1, keepdims=True) + EPS)
+        upper = total[...] * gain[...]
+        xhat = values * inv_rms
+        out_ref[...] = (
+            inv_rms * (upper - xhat * jnp.mean(upper * xhat, axis=1, keepdims=True))
+        ).astype(jnp.bfloat16)
+        sends.finish()
+
+    sends = Sends()
+
+    @pl.when(is_edge)
+    def _():
+        source = jnp.where(z == 0, 0, 1)
+        compute(zs[0])
+        line_a(0, False)
+        step1(0, zs[0], b_cols)
+        compute(zs[1])
+        line_a(1, False)
+        step1(1, zs[1], b_cols)
+        compute(zs[2])
+        compute(z)
+        step2(0, zs[0], b_cols)
+        step1(2, zs[2], b_cols)
+        step2(1, zs[1], b_cols)
+        step3(0, False)
+        line_a(2, False)
+        step1(3, z, b_cols)
+        step2(2, zs[2], b_cols)
+        step3(1, False)
+        add_a(source, z)
+        step1(4, z, a_cols)
+        step2(3, z, b_cols)
+        step2(4, z, a_cols)
+        step3(2, False)
+        finish([source])
+
+    sends = Sends()
+
+    @pl.when(jnp.logical_not(is_edge))
+    def _():
+        compute(zs[0])
+        step1(0, zs[0], b_cols)
+        compute(zs[1])
+        step1(1, zs[1], b_cols)
+        compute(zs[2])
+        compute(z)
+        step2(0, zs[0], b_cols)
+        step1(2, zs[2], b_cols)
+        line_a(0, True)
+        step2(1, zs[1], b_cols)
+        step1(3, z, b_cols)
+        line_a(1, True)
+        step2(2, zs[2], b_cols)
+        line_a(2, True)
+        step3(0, True)
+        step2(3, z, b_cols)
+        add_a(0, z)
+        add_a(1, z)
+        step1(4, z, a_cols)
+        step3(2, True)
+        step3(1, True)
+        step2(4, z, a_cols)
+        finish([0, 1])
+
+    @pl.when(s > 0)
+    def _():
+        for copy in near_back:
+            copy.wait_send()
+
+    @pl.when(s > 1)
+    def _():
+        far_back.wait_send()
+
+    @pl.when(s + 1 < blocks)
+    def _():
+        for k in range(NZ):
+            near_copy(k, zs[NZ - 1 - k]).wait_send()
+
+    @pl.when(s + 2 < blocks)
+    def _():
+        for k in range(NZ):
+            far_copy(k, zs[NZ - 1 - k]).wait_send()
 
 
 def on_device(tokens, norm_gain, query_weight, key_matrix, value_matrix, output_grad):
@@ -560,6 +688,7 @@
             vmem(low, rows, width),
             vmem(full, 1, width),
             vmem(low, width, cols),
+            vmem(low, cols, width),
             vmem(low, NZ, NX * rows, width),
             vmem(low, NX, hd, q_cols),
             vmem(low, NX, hd, q_cols),
@@ -568,8 +697,8 @@
             vmem(full, NX, 6, hd, 2 * hd),
             vmem(full, NX, 6, hd, 2 * hd),
             vmem(full, NX, 6, hd, 2 * hd),
-            vmem(low, 6 * hd, 2 * hd),
-            vmem(full, 9, hd, 2 * k_cols),
+            vmem(low, NX, 6 * hd, 2 * hd),
+            vmem(full, NX, hd, 2 * k_cols),
             vmem(low, 5, hd, 2 * k_cols),
             vmem(low, NX, hd, 2 * k_cols),
             vmem(low, hd, 2 * k_cols),
@@ -584,8 +713,8 @@
             dma((2, NZ, NX, 2)),
             dma((2, NZ)),
             dma((NZ,)),
-            dma((2, NZ)),
-            dma((NZ,)),
+            dma((2, NZ, NX)),
+            dma((NZ, NX)),
             dma((NZ,)),
             dma((NZ,)),
             dma((NZ,)),

time: 118 us -> 109 us (0.924)
  the two profiles are of different devices: /device:TPU:1 before, /device:TPU:57 now
where the time goes in v3:
time: 109 us
  Pallas kernels  106 us (97%)
  local copies, waits for them, and re-layouts  3.04 us (3%)
    pallas_call x1, Pallas kernels, on_device(): pl.pallas_call(whole, out_shape=jax.ShapeDtypeStruct((rows, width), low),...  106 us

profile of v3, /device:TPU:57, one launch (start us, length us, event | category | flops | bytes accessed | tf_op | source)
XLA Modules:
  0.0 108.8 jit_solution(1594797655938566413)
XLA Ops:
  0.0 1.3 %reshape.6.gain_ref = f32[1,4608]{1,0:T(1,128)} reshape(f32[4608]{0:T(1024)} %param.7) | data formatting | bytes 36864 | tf_op jit(solution)/shard_map/reshape | solution.py:740
  1.3 105.7 %shard_map.64 = bf16[32,4608]{1,0:T(8,128)(2,1)} custom-call(bf16[32,4608]{1,0:T(8,128)(2,1)} %tokens_ref.1, f32[1,4608]{1,0:T(1,128)} %reshape.6.gain_ref, bf16[4,128,256]{2,1,0:T(8,128)(2,1)} %bitcast.1, bf16[4608,256]{1,0:T(8,128)(2,1)} %wq_ref.1, bf16[4608,128]{1,0:T(8,128)(2,1)} %wk_ref.1, bf16[4608,128]{1,0:T(8,128)(2,1)} %wv_ref.1), custom_call_target="tpu_custom_call" | custom-call | tf_op jit(solution)/shard_map/pallas_call | solution.py:682
  107.1 1.7 %copy.8 = bf16[32,4608]{1,0:T(8,128)(2,1)} copy(bf16[32,4608]{1,0:T(8,128)(2,1)} %shard_map.64) | data formatting | bytes 589824

commit v4 on v3

--- a/solution.py
+++ b/solution.py
@@ -13,7 +13,8 @@
 MESH = pl.DeviceIdType.MESH
 NX = 4
 NZ = 4
-A_TILES = 8
+A_TILES = 5
+B_TILES = 8
 TURN = 512
 TURNS = 9
 
@@ -126,9 +127,13 @@
         load.start()
     loads[0].wait()
     loads[1].wait()
+
+    def gain_row():
+        return jnp.concatenate([gain[i : i + 1, :] for i in range(gain.shape[0])], axis=1)
+
     values = tok[...].astype(jnp.float32)
     inv_rms = lax.rsqrt(jnp.mean(values * values, axis=1, keepdims=True) + EPS)
-    g[z, pl.ds(x * rows, rows), :] = (values * inv_rms * gain[...]).astype(jnp.bfloat16)
+    g[z, pl.ds(x * rows, rows), :] = (values * inv_rms * gain_row()).astype(jnp.bfloat16)
     pl.semaphore_wait(barrier, partners)
     sends = Sends()
 
@@ -472,7 +477,10 @@
 
     zs = zs[::-1]
     p = g
-    tile = 512
+    tile = 768
+    a_width = B_TILES * 128
+    a_cols = pl.ds(0, a_width)
+    b_cols = pl.ds(a_width, width - a_width)
 
     def row_ds(xr, h=None):
         if h is None:
@@ -482,9 +490,8 @@
     def compute(zr):
         lhs = grads[:, pl.ds(pl.multiple_of(zr * rows, rows), rows), :].reshape(NX * rows, -1)
 
-        @pl.loop(0, width // tile)
-        def _(j):
-            at = pl.ds(pl.multiple_of(j * tile, tile), tile)
+        for j in range(width // tile):
+            at = pl.ds(j * tile, tile)
             p[zr, :, at] = jnp.dot(
                 lhs, wt[:, at], preferred_element_type=jnp.float32
             ).astype(jnp.bfloat16)
@@ -564,7 +571,7 @@
             p[zr, :, a_cols].astype(jnp.float32) + got_za[d, zr].astype(jnp.float32)
         ).astype(jnp.bfloat16)
 
-    def line_a(k, far):
+    def line_a(k, far, when=None):
         zr = zs[k]
         if far:
             add_a(way(zr), zr)
@@ -572,7 +579,8 @@
             send_to(
                 p.at[zr, :, a_cols], got_za.at[way(zr), zr], tza.at[k],
                 uza.at[way(zr), zr], nearer(zr),
-            )
+            ),
+            when,
         )
 
     def finish(sources):
@@ -583,7 +591,7 @@
         total[:, a_cols] = x_sum(4, z, a_cols)
         values = tok[...].astype(jnp.float32)
         inv_rms = lax.rsqrt(jnp.mean(values * values, axis=1, keepdims=True) + EPS)
-        upper = total[...] * gain[...]
+        upper = total[...] * gain_row()
         xhat = values * inv_rms
         out_ref[...] = (
             inv_rms * (upper - xhat * jnp.mean(upper * xhat, axis=1, keepdims=True))
@@ -591,18 +599,19 @@
         sends.finish()
 
     sends = Sends()
+    compute(zs[0])
+    step1(0, zs[0], b_cols)
+    line_a(0, False, is_edge)
+    compute(zs[1])
+    step1(1, zs[1], b_cols)
+    line_a(1, False, is_edge)
+    compute(zs[2])
+    compute(z)
+    opening, sends = sends, Sends()
 
     @pl.when(is_edge)
     def _():
         source = jnp.where(z == 0, 0, 1)
-        compute(zs[0])
-        line_a(0, False)
-        step1(0, zs[0], b_cols)
-        compute(zs[1])
-        line_a(1, False)
-        step1(1, zs[1], b_cols)
-        compute(zs[2])
-        compute(z)
         step2(0, zs[0], b_cols)
         step1(2, zs[2], b_cols)
         step2(1, zs[1], b_cols)
@@ -622,12 +631,6 @@
 
     @pl.when(jnp.logical_not(is_edge))
     def _():
-        compute(zs[0])
-        step1(0, zs[0], b_cols)
-        compute(zs[1])
-        step1(1, zs[1], b_cols)
-        compute(zs[2])
-        compute(z)
         step2(0, zs[0], b_cols)
         step1(2, zs[2], b_cols)
         line_a(0, True)
@@ -646,6 +649,8 @@
         step2(4, z, a_cols)
         finish([0, 1])
 
+    opening.finish()
+
     @pl.when(s > 0)
     def _():
         for copy in near_back:
@@ -670,9 +675,9 @@
     rows, width = tokens.shape
     q_cols, k_cols = query_weight.shape[1], key_matrix.shape[1]
     cols = q_cols + 2 * k_cols
-    a_width = A_TILES * 128
+    a_width = B_TILES * 128
     hd = HEAD_SIZE
-    any_space = pl.BlockSpec(memory_space=pl.ANY)
+    any_space = pl.BlockSpec(memory_space=pltpu.HBM)
     dma = pltpu.SemaphoreType.DMA
     low, full = jnp.bfloat16, jnp.float32
 
@@ -686,7 +691,7 @@
         out_specs=pl.BlockSpec(memory_space=pltpu.VMEM),
         scratch_shapes=[
             vmem(low, rows, width),
-            vmem(full, 1, width),
+            vmem(full, width // 128, 128),
             vmem(low, width, cols),
             vmem(low, cols, width),
             vmem(low, NZ, NX * rows, width),
@@ -737,7 +742,7 @@
         ),
     )(
         tokens,
-        norm_gain.reshape(1, -1),
+        norm_gain.reshape(-1, 128),
         output_grad.reshape(NX, hd, q_cols),
         query_weight,
         key_matrix,

time: 109 us -> 102 us (0.936)
  the two profiles are of different devices: /device:TPU:57 before, /device:TPU:33 now
where the time goes in v4:
time: 102 us
  Pallas kernels  100 us (98%)
  local copies, waits for them, and re-layouts  1.69 us (2%)
    pallas_call x1, Pallas kernels, on_device(): pl.pallas_call(whole, out_shape=jax.ShapeDtypeStruct((rows, width), low),...  100 us

profile of v4, /device:TPU:33, one launch (start us, length us, event | category | flops | bytes accessed | tf_op | source)
XLA Modules:
  0.0 102.2 jit_solution(7005192574776022110)
XLA Ops:
  0.0 100.5 %shard_map.64 = bf16[32,4608]{1,0:T(8,128)(2,1)} custom-call(bf16[32,4608]{1,0:T(8,128)(2,1)} %tokens_ref.1, f32[36,128]{1,0:T(8,128)} %bitcast.3, bf16[4,128,256]{2,1,0:T(8,128)(2,1)} %bitcast.2, bf16[4608,256]{1,0:T(8,128)(2,1)} %wq_ref.1, bf16[4608,128]{1,0:T(8,128)(2,1)} %wk_ref.1, bf16[4608,128]{1,0:T(8,128)(2,1)} %wv_ref.1), custom_call_target="tpu_custom_call" | custom-call | tf_op jit(solution)/shard_map/pallas_call | solution.py:687
  100.5 1.7 %copy.8 = bf16[32,4608]{1,0:T(8,128)(2,1)} copy(bf16[32,4608]{1,0:T(8,128)(2,1)} %shard_map.64) | data formatting | bytes 589824

commit v5 on v4

--- a/solution.py
+++ b/solution.py
@@ -59,22 +59,33 @@
     )
 
 
-def greet_partners(x, z, s, blocks):
+def greet(device):
     barrier = pltpu.get_barrier_semaphore()
-
-    def greet(device):
-        pl.semaphore_signal(barrier, inc=1, device_id=device, device_id_type=MESH)
-
+    pl.semaphore_signal(barrier, inc=1, device_id=device, device_id_type=MESH)
+
+
+def meet(x, z, s, blocks):
+    barrier = pltpu.get_barrier_semaphore()
+    early = (s // 2) % 2 == 0
     greet({"tp": tp_of((x + 1) % NX, z)})
     greet({"tp": tp_of((x + 3) % NX, z)})
     pl.when(z > 0)(lambda: greet({"tp": tp_of(x, z - 1)}))
     pl.when(z < NZ - 1)(lambda: greet({"tp": tp_of(x, z + 1)}))
-    count = jnp.where((z == 0) | (z == NZ - 1), 3, 4)
-    for step in (-2, -1, 1, 2):
-        there = (s + step >= 0) & (s + step < blocks)
-        pl.when(there)(lambda step=step: greet({"seq": s + step}))
-        count = count + jnp.where(there, 1, 0)
-    return barrier, count
+    greet({"seq": s + 1 - 2 * (s % 2)})
+    near = jnp.where((z == 0) | (z == NZ - 1), 4, 5)
+    others = [s - 2, s + 2, s - 1 + 2 * (s % 2)]
+    there = [(o >= 0) & (o < blocks) for o in others]
+    far = sum(jnp.where(t, 1, 0) for t in there)
+
+    def first():
+        pl.semaphore_wait(barrier, near + jnp.where(early, 0, far))
+        for o, t in zip(others, there):
+            pl.when(t)(lambda o=o: greet({"seq": o}))
+
+    def second():
+        pl.when(early)(lambda: pl.semaphore_wait(barrier, far))
+
+    return first, second
 
 
 class Sends:
@@ -114,7 +125,7 @@
     xp, xm, xo = (x + 1) % NX, (x + 3) % NX, (x + 2) % NX
     zs = near_to_far(z)
     q_cols, k_cols = wq_ref.shape[1], wk_ref.shape[1]
-    barrier, partners = greet_partners(x, z, s, blocks)
+    meet_first, meet_second = meet(x, z, s, blocks)
     loads = [
         pltpu.make_async_copy(tokens_ref, tok, load_sem.at[0]),
         pltpu.make_async_copy(gain_ref, gain, load_sem.at[1]),
@@ -134,7 +145,7 @@
     values = tok[...].astype(jnp.float32)
     inv_rms = lax.rsqrt(jnp.mean(values * values, axis=1, keepdims=True) + EPS)
     g[z, pl.ds(x * rows, rows), :] = (values * inv_rms * gain_row()).astype(jnp.bfloat16)
-    pl.semaphore_wait(barrier, partners)
+    meet_first()
     sends = Sends()
 
     def part(zr, xr, h, cols):
@@ -247,6 +258,7 @@
         x_rest_opposite(NZ, z, a_cols)
         z_send_a(0, z, xo, way, to)
         x_forward(0, z, b_cols)
+        meet_second()
 
     def clear_edges():
         @pl.when(s == 0)
@@ -481,6 +493,8 @@
     a_width = B_TILES * 128
     a_cols = pl.ds(0, a_width)
     b_cols = pl.ds(a_width, width - a_width)
+    b_half = (width - a_width) // 2
+    b_parts = [pl.ds(a_width, b_half), pl.ds(a_width + b_half, b_half)]
 
     def row_ds(xr, h=None):
         if h is None:
@@ -514,38 +528,47 @@
                 )
             )
 
-    def step2(k, zr, cols):
+    def step2(k, zr, parts):
         for direction, to in ((0, xm), (1, xp)):
-            land = got_opp.at[direction, zr, :, cols]
-            send_to(land, land, s1.at[direction, k], r1.at[direction, k], tp_of(to, z)).wait_recv()
+            for cols in parts if len(parts) == 1 else [b_cols]:
+                land = got_opp.at[direction, zr, :, cols]
+                send_to(
+                    land, land, s1.at[direction, k], r1.at[direction, k], tp_of(to, z)
+                ).wait_recv()
             at = row_ds(to, direction)
-            p[zr, at, cols] = (
-                p[zr, at, cols].astype(jnp.float32)
-                + got_opp[direction, zr, :, cols].astype(jnp.float32)
-            ).astype(jnp.bfloat16)
-            sends.start(
-                send_to(
-                    p.at[zr, row_ds(to), cols],
-                    got_x.at[direction, zr, :, cols],
-                    s2.at[direction, k],
-                    r2.at[direction, k],
-                    tp_of(to, z),
+            for h, cols in enumerate(parts):
+                p[zr, at, cols] = (
+                    p[zr, at, cols].astype(jnp.float32)
+                    + got_opp[direction, zr, :, cols].astype(jnp.float32)
+                ).astype(jnp.bfloat16)
+                sends.start(
+                    send_to(
+                        p.at[zr, row_ds(to), cols],
+                        got_x.at[direction, zr, :, cols],
+                        s2.at[direction, k, h],
+                        r2.at[direction, k, h],
+                        tp_of(to, z),
+                    )
                 )
-            )
-
-    def x_sum(k, zr, cols):
+
+    def x_sum(k, h, zr, cols):
         for direction, to in ((0, xm), (1, xp)):
             land = got_x.at[direction, zr, :, cols]
-            send_to(land, land, s2.at[direction, k], r2.at[direction, k], tp_of(to, z)).wait_recv()
+            send_to(
+                land, land, s2.at[direction, k, h], r2.at[direction, k, h], tp_of(to, z)
+            ).wait_recv()
         return (
             p[zr, row_ds(x), cols].astype(jnp.float32)
             + got_x[0, zr, :, cols].astype(jnp.float32)
             + got_x[1, zr, :, cols].astype(jnp.float32)
         )
 
-    def line_wait_b(d, zr):
-        land = got_zb.at[d, zr]
-        send_to(land, land, tzb.at[0], uzb.at[d, zr], tp_of(xp, z)).wait_recv()
+    def line_b(d, zr, h):
+        return got_zb.at[d, zr, h]
+
+    def line_wait_b(d, zr, h):
+        land = line_b(d, zr, h)
+        send_to(land, land, tzb.at[0, h], uzb.at[d, zr, h], tp_of(xp, z)).wait_recv()
 
     def line_wait_a(d, zr):
         land = got_za.at[d, zr]
@@ -553,17 +576,18 @@
 
     def step3(k, far):
         zr = zs[k]
-        value = x_sum(k, zr, b_cols)
-        if far:
-            line_wait_b(way(zr), zr)
-            value = value + got_zb[way(zr), zr].astype(jnp.float32)
-        p[zr, row_ds(x), b_cols] = value.astype(jnp.bfloat16)
-        sends.start(
-            send_to(
-                p.at[zr, row_ds(x), b_cols], got_zb.at[way(zr), zr], tzb.at[k],
-                uzb.at[way(zr), zr], nearer(zr),
+        for h, cols in enumerate(b_parts):
+            value = x_sum(k, h, zr, cols)
+            if far:
+                line_wait_b(way(zr), zr, h)
+                value = value + got_zb[way(zr), zr, h].astype(jnp.float32)
+            p[zr, row_ds(x), cols] = value.astype(jnp.bfloat16)
+            sends.start(
+                send_to(
+                    p.at[zr, row_ds(x), cols], line_b(way(zr), zr, h), tzb.at[k, h],
+                    uzb.at[way(zr), zr, h], nearer(zr),
+                )
             )
-        )
 
     def add_a(d, zr):
         line_wait_a(d, zr)
@@ -584,11 +608,13 @@
         )
 
     def finish(sources):
-        total[:, b_cols] = x_sum(3, z, b_cols)
-        for d in sources:
-            line_wait_b(d, z)
-            total[:, b_cols] = total[:, b_cols] + got_zb[d, z].astype(jnp.float32)
-        total[:, a_cols] = x_sum(4, z, a_cols)
+        for h, cols in enumerate(b_parts):
+            value = x_sum(3, h, z, cols)
+            for d in sources:
+                line_wait_b(d, z, h)
+                value = value + got_zb[d, z, h].astype(jnp.float32)
+            total[:, cols] = value
+        total[:, a_cols] = x_sum(4, 0, z, a_cols)
         values = tok[...].astype(jnp.float32)
         inv_rms = lax.rsqrt(jnp.mean(values * values, axis=1, keepdims=True) + EPS)
         upper = total[...] * gain_row()
@@ -606,47 +632,47 @@
     step1(1, zs[1], b_cols)
     line_a(1, False, is_edge)
     compute(zs[2])
+    line_a(2, False, is_edge)
     compute(z)
     opening, sends = sends, Sends()
 
     @pl.when(is_edge)
     def _():
         source = jnp.where(z == 0, 0, 1)
-        step2(0, zs[0], b_cols)
+        step2(0, zs[0], b_parts)
         step1(2, zs[2], b_cols)
-        step2(1, zs[1], b_cols)
+        step2(1, zs[1], b_parts)
+        step1(3, z, b_cols)
+        step2(2, zs[2], b_parts)
         step3(0, False)
-        line_a(2, False)
-        step1(3, z, b_cols)
-        step2(2, zs[2], b_cols)
         step3(1, False)
+        step2(3, z, b_parts)
         add_a(source, z)
         step1(4, z, a_cols)
-        step2(3, z, b_cols)
-        step2(4, z, a_cols)
         step3(2, False)
+        step2(4, z, [a_cols])
         finish([source])
 
     sends = Sends()
 
     @pl.when(jnp.logical_not(is_edge))
     def _():
-        step2(0, zs[0], b_cols)
+        step2(0, zs[0], b_parts)
         step1(2, zs[2], b_cols)
         line_a(0, True)
-        step2(1, zs[1], b_cols)
+        step2(1, zs[1], b_parts)
         step1(3, z, b_cols)
         line_a(1, True)
-        step2(2, zs[2], b_cols)
+        step2(2, zs[2], b_parts)
         line_a(2, True)
         step3(0, True)
-        step2(3, z, b_cols)
+        step2(3, z, b_parts)
         add_a(0, z)
         add_a(1, z)
         step1(4, z, a_cols)
         step3(2, True)
         step3(1, True)
-        step2(4, z, a_cols)
+        step2(4, z, [a_cols])
         finish([0, 1])
 
     opening.finish()
@@ -712,7 +738,7 @@
             vmem(low, 2, NZ, rows // 2, width),
             vmem(low, 2, NZ, rows, width),
             vmem(low, 2, NZ, NX * rows, a_width),
-            vmem(low, 2, NZ, rows, width - a_width),
+            vmem(low, 2, NZ, 2, rows, (width - a_width) // 2),
             dma((6,)),
             dma((2, NZ + 1, 3)),
             dma((2, NZ, NX, 2)),
@@ -730,12 +756,12 @@
             dma((1,)),
             dma((2, NZ + 1)),
             dma((2, NZ + 1)),
-            dma((2, NZ + 1)),
-            dma((2, NZ + 1)),
+            dma((2, NZ + 1, 2)),
+            dma((2, NZ + 1, 2)),
             dma((NZ,)),
             dma((2, NZ)),
-            dma((NZ,)),
-            dma((2, NZ)),
+            dma((NZ, 2)),
+            dma((2, NZ, 2)),
         ],
         compiler_params=pltpu.CompilerParams(
             collective_id=0, has_side_effects=True, vmem_limit_bytes=62 * 1024 * 1024

time: 102 us -> 99.9 us (0.979)
  the two profiles are of different devices: /device:TPU:33 before, /device:TPU:193 now
where the time goes in v5:
time: 99.9 us; the launch traced here: 99.8 us
  Pallas kernels  98.1 us (98%)
  local copies, waits for them, and re-layouts  1.69 us (2%)
    pallas_call x1, Pallas kernels, on_device(): pl.pallas_call(whole, out_shape=jax.ShapeDtypeStruct((rows, width), low),...  98.1 us

profile of v5, /device:TPU:193, one launch (start us, length us, event | category | flops | bytes accessed | tf_op | source)
XLA Modules:
  0.0 99.8 jit_solution(3497410275182449349)
XLA Ops:
  0.0 98.1 %shard_map.64 = bf16[32,4608]{1,0:T(8,128)(2,1)} custom-call(bf16[32,4608]{1,0:T(8,128)(2,1)} %tokens_ref.1, f32[36,128]{1,0:T(8,128)} %bitcast.3, bf16[4,128,256]{2,1,0:T(8,128)(2,1)} %bitcast.2, bf16[4608,256]{1,0:T(8,128)(2,1)} %wq_ref.1, bf16[4608,128]{1,0:T(8,128)(2,1)} %wk_ref.1, bf16[4608,128]{1,0:T(8,128)(2,1)} %wv_ref.1), custom_call_target="tpu_custom_call" | custom-call | tf_op jit(solution)/shard_map/pallas_call | solution.py:713
  98.1 1.7 %copy.8 = bf16[32,4608]{1,0:T(8,128)(2,1)} copy(bf16[32,4608]{1,0:T(8,128)(2,1)} %shard_map.64) | data formatting | bytes 589824

commit v6 on v5

--- a/solution.py
+++ b/solution.py
@@ -110,9 +110,9 @@
 def whole(
     tokens_ref, gain_ref, grad_ref, wq_ref, wk_ref, wv_ref, out_ref,
     tok, gain, w, wt, g, dout, qb, kv, kt, e_buf, dp_buf, b_buf, dr_buf, acc,
-    back_out, back_near, back_far, grads, total, got_opp, got_x, got_za, got_zb,
+    back_out, back_near, back_far, back_chip, grads, total, got_opp, got_x, got_za, got_zb,
     load_sem, sx, rx, szb, rzb, sza, rza, s_near, r_near, s_far, r_far,
-    s_bn, r_bn, s_bf, r_bf, s1, r1, s2, r2, tza, uza, tzb, uzb,
+    s_bn, r_bn, s_bf, r_bf, s_bc, r_bc, s1, r1, s2, r2, tza, uza, tzb, uzb,
 ):
     x, z = place()
     s = lax.axis_index("seq")
@@ -234,8 +234,8 @@
         for i in range(NX):
             kv[5 + i, at, :] = out[i * rows : (i + 1) * rows, q_cols:]
             qb[i, at, :] = out[i * rows : (i + 1) * rows, :q_cols]
+        pl.when(s + 2 < blocks)(lambda: far_copy(k, zr).start())
         pl.when(s + 1 < blocks)(lambda: near_copy(k, zr).start())
-        pl.when(s + 2 < blocks)(lambda: far_copy(k, zr).start())
 
     is_edge = (z == 0) | (z == NZ - 1)
 
@@ -273,7 +273,7 @@
         def _():
             back_near[...] = jnp.zeros_like(back_near)
 
-        @pl.when(s >= blocks - 2)
+        @pl.when((s >= blocks - 2) | (s % 2 == 1))
         def _():
             back_far[...] = jnp.zeros_like(back_far)
 
@@ -451,14 +451,31 @@
         )
         for j in range(1, 5)
     ]
+    chip_back = send_along(
+        back_out.at[0], back_chip, s_bc.at[0], r_bc.at[0], jnp.maximum(s - 1, 0)
+    )
+    is_odd = s % 2 == 1
     for j in range(5):
         d_key, d_value = tile_grads(j)
         back_out[j, :, 0:hd] = d_key.astype(jnp.bfloat16)
         back_out[j, :, hd : 2 * hd] = d_value.astype(jnp.bfloat16)
         if j == 0:
-            pl.when(s > 1)(lambda: far_back.start())
+            pl.when(is_odd)(lambda: chip_back.start())
+        elif j < 4:
+            pl.when(s > 0)(lambda j=j: near_back[j - 1].start())
         else:
-            pl.when(s > 0)(lambda j=j: near_back[j - 1].start())
+
+            @pl.when(jnp.logical_not(is_odd))
+            def _():
+                chip_back.wait_recv()
+                other = back_chip[...].astype(jnp.float32)
+                back_out[j, :, 0:hd] = (d_key + other[:, 0:hd]).astype(jnp.bfloat16)
+                back_out[j, :, hd : 2 * hd] = (d_value + other[:, hd : 2 * hd]).astype(
+                    jnp.bfloat16
+                )
+
+            pl.when(s > 0)(lambda: near_back[3].start())
+            pl.when((s > 1) & jnp.logical_not(is_odd))(lambda: far_back.start())
     for j in range(5, 9):
         d_key, d_value = tile_grads(j)
         acc[j - 5, :, 0:hd] = d_key
@@ -470,9 +487,9 @@
         grads[qt, :, 0:hd] = d_query[:, 0:hd].T.astype(jnp.bfloat16)
         grads[qt, :, hd : 2 * hd] = d_query[:, hd : 2 * hd].T.astype(jnp.bfloat16)
 
-    @pl.when(s < blocks - 2)
-    def _():
-        send_along(back_out.at[0], back_far, s_bf.at[0], r_bf.at[0], s).wait_recv()
+    @pl.when((s < blocks - 2) & jnp.logical_not(is_odd))
+    def _():
+        far_back.wait_recv()
 
     @pl.when(s < blocks - 1)
     def _():
@@ -494,6 +511,8 @@
     a_cols = pl.ds(0, a_width)
     b_cols = pl.ds(a_width, width - a_width)
     b_half = (width - a_width) // 2
+    a_half = a_width // 2
+    a_parts = [pl.ds(0, a_half), pl.ds(a_half, a_half)]
     b_parts = [pl.ds(a_width, b_half), pl.ds(a_width + b_half, b_half)]
 
     def row_ds(xr, h=None):
@@ -570,9 +589,9 @@
         land = line_b(d, zr, h)
         send_to(land, land, tzb.at[0, h], uzb.at[d, zr, h], tp_of(xp, z)).wait_recv()
 
-    def line_wait_a(d, zr):
-        land = got_za.at[d, zr]
-        send_to(land, land, tza.at[0], uza.at[d, zr], tp_of(xp, z)).wait_recv()
+    def line_wait_a(d, zr, h):
+        land = got_za.at[d, zr, :, a_parts[h]]
+        send_to(land, land, tza.at[0, h], uza.at[d, zr, h], tp_of(xp, z)).wait_recv()
 
     def step3(k, far):
         zr = zs[k]
@@ -589,23 +608,25 @@
                 )
             )
 
-    def add_a(d, zr):
-        line_wait_a(d, zr)
-        p[zr, :, a_cols] = (
-            p[zr, :, a_cols].astype(jnp.float32) + got_za[d, zr].astype(jnp.float32)
+    def add_a(d, zr, h):
+        line_wait_a(d, zr, h)
+        cols = a_parts[h]
+        p[zr, :, cols] = (
+            p[zr, :, cols].astype(jnp.float32) + got_za[d, zr, :, cols].astype(jnp.float32)
         ).astype(jnp.bfloat16)
 
     def line_a(k, far, when=None):
         zr = zs[k]
-        if far:
-            add_a(way(zr), zr)
-        sends.start(
-            send_to(
-                p.at[zr, :, a_cols], got_za.at[way(zr), zr], tza.at[k],
-                uza.at[way(zr), zr], nearer(zr),
-            ),
-            when,
-        )
+        for h, cols in enumerate(a_parts):
+            if far:
+                add_a(way(zr), zr, h)
+            sends.start(
+                send_to(
+                    p.at[zr, :, cols], got_za.at[way(zr), zr, :, cols], tza.at[k, h],
+                    uza.at[way(zr), zr, h], nearer(zr),
+                ),
+                when,
+            )
 
     def finish(sources):
         for h, cols in enumerate(b_parts):
@@ -646,9 +667,10 @@
         step2(2, zs[2], b_parts)
         step3(0, False)
         step3(1, False)
+        add_a(source, z, 0)
+        add_a(source, z, 1)
+        step1(4, z, a_cols)
         step2(3, z, b_parts)
-        add_a(source, z)
-        step1(4, z, a_cols)
         step3(2, False)
         step2(4, z, [a_cols])
         finish([source])
@@ -665,11 +687,12 @@
         line_a(1, True)
         step2(2, zs[2], b_parts)
         line_a(2, True)
+        for d in (0, 1):
+            for h in (0, 1):
+                add_a(d, z, h)
+        step1(4, z, a_cols)
+        step2(3, z, b_parts)
         step3(0, True)
-        step2(3, z, b_parts)
-        add_a(0, z)
-        add_a(1, z)
-        step1(4, z, a_cols)
         step3(2, True)
         step3(1, True)
         step2(4, z, [a_cols])
@@ -682,9 +705,13 @@
         for copy in near_back:
             copy.wait_send()
 
-    @pl.when(s > 1)
+    @pl.when((s > 1) & jnp.logical_not(is_odd))
     def _():
         far_back.wait_send()
+
+    @pl.when(is_odd)
+    def _():
+        chip_back.wait_send()
 
     @pl.when(s + 1 < blocks)
     def _():
@@ -733,6 +760,7 @@
             vmem(low, 5, hd, 2 * k_cols),
             vmem(low, NX, hd, 2 * k_cols),
             vmem(low, hd, 2 * k_cols),
+            vmem(low, hd, 2 * k_cols),
             vmem(low, NX, hd, cols),
             vmem(full, rows, width),
             vmem(low, 2, NZ, rows // 2, width),
@@ -754,12 +782,14 @@
             dma((NX,)),
             dma((1,)),
             dma((1,)),
+            dma((1,)),
+            dma((1,)),
             dma((2, NZ + 1)),
             dma((2, NZ + 1)),
             dma((2, NZ + 1, 2)),
             dma((2, NZ + 1, 2)),
-            dma((NZ,)),
-            dma((2, NZ)),
+            dma((NZ, 2)),
+            dma((2, NZ, 2)),
             dma((NZ, 2)),
             dma((2, NZ, 2)),
         ],

time: 99.9 us -> 102 us (1.021)
  the two profiles are of different devices: /device:TPU:193 before, /device:TPU:24 now
where the time goes in v6:
time: 102 us; the launch traced here: 100 us
  Pallas kernels  98.3 us (96%)
  local copies, waits for them, and re-layouts  1.69 us (2%)
    pallas_call x1, Pallas kernels, on_device(): pl.pallas_call(whole, out_shape=jax.ShapeDtypeStruct((rows, width), low),...  98.3 us

profile of v6, /device:TPU:24, one launch (start us, length us, event | category | flops | bytes accessed | tf_op | source)
XLA Modules:
  0.0 100.0 jit_solution(10748171662198034547)
XLA Ops:
  0.0 98.3 %shard_map.64 = bf16[32,4608]{1,0:T(8,128)(2,1)} custom-call(bf16[32,4608]{1,0:T(8,128)(2,1)} %tokens_ref.1, f32[36,128]{1,0:T(8,128)} %bitcast.3, bf16[4,128,256]{2,1,0:T(8,128)(2,1)} %bitcast.2, bf16[4608,256]{1,0:T(8,128)(2,1)} %wq_ref.1, bf16[4608,128]{1,0:T(8,128)(2,1)} %wk_ref.1, bf16[4608,128]{1,0:T(8,128)(2,1)} %wv_ref.1), custom_call_target="tpu_custom_call" | custom-call | tf_op jit(solution)/shard_map/pallas_call | solution.py:740
  98.3 1.7 %copy.8 = bf16[32,4608]{1,0:T(8,128)(2,1)} copy(bf16[32,4608]{1,0:T(8,128)(2,1)} %shard_map.64) | data formatting | bytes 589824

commit v7 on v6

--- a/solution.py
+++ b/solution.py
@@ -461,6 +461,7 @@
         back_out[j, :, hd : 2 * hd] = d_value.astype(jnp.bfloat16)
         if j == 0:
             pl.when(is_odd)(lambda: chip_back.start())
+            pl.when((s > 1) & jnp.logical_not(is_odd))(lambda: far_back.start())
         elif j < 4:
             pl.when(s > 0)(lambda j=j: near_back[j - 1].start())
         else:
@@ -475,7 +476,6 @@
                 )
 
             pl.when(s > 0)(lambda: near_back[3].start())
-            pl.when((s > 1) & jnp.logical_not(is_odd))(lambda: far_back.start())
     for j in range(5, 9):
         d_key, d_value = tile_grads(j)
         acc[j - 5, :, 0:hd] = d_key
@@ -691,8 +691,8 @@
             for h in (0, 1):
                 add_a(d, z, h)
         step1(4, z, a_cols)
+        step3(0, True)
         step2(3, z, b_parts)
-        step3(0, True)
         step3(2, True)
         step3(1, True)
         step2(4, z, [a_cols])

time: 102 us -> 98.8 us (0.969)
  the two profiles are of different devices: /device:TPU:24 before, /device:TPU:40 now
where the time goes in v7:
time: 98.8 us; the launch traced here: 98.7 us
  Pallas kernels  97 us (98%)
  local copies, waits for them, and re-layouts  1.69 us (2%)
    pallas_call x1, Pallas kernels, on_device(): pl.pallas_call(whole, out_shape=jax.ShapeDtypeStruct((rows, width), low),...  97 us

profile of v7, /device:TPU:40, one launch (start us, length us, event | category | flops | bytes accessed | tf_op | source)
XLA Modules:
  0.0 98.7 jit_solution(10570727942205177511)
XLA Ops:
  0.0 97.0 %shard_map.64 = bf16[32,4608]{1,0:T(8,128)(2,1)} custom-call(bf16[32,4608]{1,0:T(8,128)(2,1)} %tokens_ref.1, f32[36,128]{1,0:T(8,128)} %bitcast.3, bf16[4,128,256]{2,1,0:T(8,128)(2,1)} %bitcast.2, bf16[4608,256]{1,0:T(8,128)(2,1)} %wq_ref.1, bf16[4608,128]{1,0:T(8,128)(2,1)} %wk_ref.1, bf16[4608,128]{1,0:T(8,128)(2,1)} %wv_ref.1), custom_call_target="tpu_custom_call" | custom-call | tf_op jit(solution)/shard_map/pallas_call | solution.py:740
  97.0 1.7 %copy.8 = bf16[32,4608]{1,0:T(8,128)(2,1)} copy(bf16[32,4608]{1,0:T(8,128)(2,1)} %shard_map.64) | data formatting | bytes 589824

commit v8 on v7

--- a/solution.py
+++ b/solution.py
@@ -661,12 +661,12 @@
     def _():
         source = jnp.where(z == 0, 0, 1)
         step2(0, zs[0], b_parts)
+        step2(1, zs[1], b_parts)
         step1(2, zs[2], b_cols)
-        step2(1, zs[1], b_parts)
         step1(3, z, b_cols)
-        step2(2, zs[2], b_parts)
         step3(0, False)
         step3(1, False)
+        step2(2, zs[2], b_parts)
         add_a(source, z, 0)
         add_a(source, z, 1)
         step1(4, z, a_cols)
@@ -680,21 +680,21 @@
     @pl.when(jnp.logical_not(is_edge))
     def _():
         step2(0, zs[0], b_parts)
+        step2(1, zs[1], b_parts)
         step1(2, zs[2], b_cols)
+        step1(3, z, b_cols)
         line_a(0, True)
-        step2(1, zs[1], b_parts)
-        step1(3, z, b_cols)
         line_a(1, True)
+        line_a(2, True)
+        step3(0, True)
         step2(2, zs[2], b_parts)
-        line_a(2, True)
         for d in (0, 1):
             for h in (0, 1):
                 add_a(d, z, h)
         step1(4, z, a_cols)
-        step3(0, True)
         step2(3, z, b_parts)
+        step3(1, True)
         step3(2, True)
-        step3(1, True)
         step2(4, z, [a_cols])
         finish([0, 1])
 

time: 98.8 us -> 101 us (1.022)
  the two profiles are of different devices: /device:TPU:40 before, /device:TPU:24 now
where the time goes in v8:
time: 101 us; the launch traced here: 100 us
  Pallas kernels  98.5 us (98%)
  local copies, waits for them, and re-layouts  1.69 us (2%)
    pallas_call x1, Pallas kernels, on_device(): pl.pallas_call(whole, out_shape=jax.ShapeDtypeStruct((rows, width), low),...  98.5 us

profile of v8, /device:TPU:24, one launch (start us, length us, event | category | flops | bytes accessed | tf_op | source)
XLA Modules:
  0.0 100.2 jit_solution(17317585740169571594)
XLA Ops:
  0.0 98.5 %shard_map.64 = bf16[32,4608]{1,0:T(8,128)(2,1)} custom-call(bf16[32,4608]{1,0:T(8,128)(2,1)} %tokens_ref.1, f32[36,128]{1,0:T(8,128)} %bitcast.3, bf16[4,128,256]{2,1,0:T(8,128)(2,1)} %bitcast.2, bf16[4608,256]{1,0:T(8,128)(2,1)} %wq_ref.1, bf16[4608,128]{1,0:T(8,128)(2,1)} %wk_ref.1, bf16[4608,128]{1,0:T(8,128)(2,1)} %wv_ref.1), custom_call_target="tpu_custom_call" | custom-call | tf_op jit(solution)/shard_map/pallas_call | solution.py:740
  98.5 1.7 %copy.8 = bf16[32,4608]{1,0:T(8,128)(2,1)} copy(bf16[32,4608]{1,0:T(8,128)(2,1)} %shard_map.64) | data formatting | bytes 589824

commit v9 on v8

--- a/solution.py
+++ b/solution.py
@@ -653,6 +653,7 @@
     step1(1, zs[1], b_cols)
     line_a(1, False, is_edge)
     compute(zs[2])
+    step1(2, zs[2], b_cols)
     line_a(2, False, is_edge)
     compute(z)
     opening, sends = sends, Sends()
@@ -662,16 +663,15 @@
         source = jnp.where(z == 0, 0, 1)
         step2(0, zs[0], b_parts)
         step2(1, zs[1], b_parts)
-        step1(2, zs[2], b_cols)
+        step2(2, zs[2], b_parts)
         step1(3, z, b_cols)
         step3(0, False)
         step3(1, False)
-        step2(2, zs[2], b_parts)
         add_a(source, z, 0)
         add_a(source, z, 1)
         step1(4, z, a_cols)
+        step3(2, False)
         step2(3, z, b_parts)
-        step3(2, False)
         step2(4, z, [a_cols])
         finish([source])
 
@@ -681,21 +681,20 @@
     def _():
         step2(0, zs[0], b_parts)
         step2(1, zs[1], b_parts)
-        step1(2, zs[2], b_cols)
+        step2(2, zs[2], b_parts)
         step1(3, z, b_cols)
         line_a(0, True)
         line_a(1, True)
         line_a(2, True)
-        step3(0, True)
-        step2(2, zs[2], b_parts)
         for d in (0, 1):
             for h in (0, 1):
                 add_a(d, z, h)
         step1(4, z, a_cols)
+        step3(0, True)
         step2(3, z, b_parts)
         step3(1, True)
+        step2(4, z, [a_cols])
         step3(2, True)
-        step2(4, z, [a_cols])
         finish([0, 1])
 
     opening.finish()

time: 101 us -> 99.5 us (0.985)
  no operation moved by 1% of the time
where the time goes in v9:
time: 99.5 us; the launch traced here: 99.4 us
  Pallas kernels  97.7 us (98%)
  local copies, waits for them, and re-layouts  1.69 us (2%)
    pallas_call x1, Pallas kernels, on_device(): pl.pallas_call(whole, out_shape=jax.ShapeDtypeStruct((rows, width), low),...  97.7 us

profile of v9, /device:TPU:24, one launch (start us, length us, event | category | flops | bytes accessed | tf_op | source)
XLA Modules:
  0.0 99.4 jit_solution(11859372781165765586)
XLA Ops:
  0.0 97.7 %shard_map.64 = bf16[32,4608]{1,0:T(8,128)(2,1)} custom-call(bf16[32,4608]{1,0:T(8,128)(2,1)} %tokens_ref.1, f32[36,128]{1,0:T(8,128)} %bitcast.3, bf16[4,128,256]{2,1,0:T(8,128)(2,1)} %bitcast.2, bf16[4608,256]{1,0:T(8,128)(2,1)} %wq_ref.1, bf16[4608,128]{1,0:T(8,128)(2,1)} %wk_ref.1, bf16[4608,128]{1,0:T(8,128)(2,1)} %wv_ref.1), custom_call_target="tpu_custom_call" | custom-call | tf_op jit(solution)/shard_map/pallas_call | solution.py:739
  97.7 1.7 %copy.8 = bf16[32,4608]{1,0:T(8,128)(2,1)} copy(bf16[32,4608]{1,0:T(8,128)(2,1)} %shard_map.64) | data formatting | bytes 589824

commit v10 on v9

--- a/solution.py
+++ b/solution.py
@@ -593,9 +593,10 @@
         land = got_za.at[d, zr, :, a_parts[h]]
         send_to(land, land, tza.at[0, h], uza.at[d, zr, h], tp_of(xp, z)).wait_recv()
 
-    def step3(k, far):
+    def step3(k, far, halves=(0, 1)):
         zr = zs[k]
-        for h, cols in enumerate(b_parts):
+        for h in halves:
+            cols = b_parts[h]
             value = x_sum(k, h, zr, cols)
             if far:
                 line_wait_b(way(zr), zr, h)
@@ -692,9 +693,10 @@
         step1(4, z, a_cols)
         step3(0, True)
         step2(3, z, b_parts)
-        step3(1, True)
+        for h in (0, 1):
+            step3(2, True, (h,))
+            step3(1, True, (h,))
         step2(4, z, [a_cols])
-        step3(2, True)
         finish([0, 1])
 
     opening.finish()

time: 99.5 us -> 98.2 us (0.987); the launches traced: 99.4 us -> 96.7 us
  Pallas kernels: 97.7 us -> 95 us
    pallas_call x1, Pallas kernels: 97.7 us -> 95 us  [on_device(): pl.pallas_call(whole, out_shape=jax.ShapeDtypeStruct((rows, width), low),...]
where the time goes in v10:
time: 98.2 us; the launch traced here: 96.7 us
  Pallas kernels  95 us (97%)
  local copies, waits for them, and re-layouts  1.69 us (2%)
    pallas_call x1, Pallas kernels, on_device(): pl.pallas_call(whole, out_shape=jax.ShapeDtypeStruct((rows, width), low),...  95 us

profile of v10, /device:TPU:24, one launch (start us, length us, event | category | flops | bytes accessed | tf_op | source)
XLA Modules:
  0.0 96.7 jit_solution(6089534254517583962)
XLA Ops:
  0.0 95.0 %shard_map.64 = bf16[32,4608]{1,0:T(8,128)(2,1)} custom-call(bf16[32,4608]{1,0:T(8,128)(2,1)} %tokens_ref.1, f32[36,128]{1,0:T(8,128)} %bitcast.3, bf16[4,128,256]{2,1,0:T(8,128)(2,1)} %bitcast.2, bf16[4608,256]{1,0:T(8,128)(2,1)} %wq_ref.1, bf16[4608,128]{1,0:T(8,128)(2,1)} %wk_ref.1, bf16[4608,128]{1,0:T(8,128)(2,1)} %wv_ref.1), custom_call_target="tpu_custom_call" | custom-call | tf_op jit(solution)/shard_map/pallas_call | solution.py:741
  95.0 1.7 %copy.8 = bf16[32,4608]{1,0:T(8,128)(2,1)} copy(bf16[32,4608]{1,0:T(8,128)(2,1)} %shard_map.64) | data formatting | bytes 589824

commit v11 on v10

--- a/solution.py
+++ b/solution.py
@@ -14,7 +14,7 @@
 NX = 4
 NZ = 4
 A_TILES = 5
-B_TILES = 8
+B_TILES = 6
 TURN = 512
 TURNS = 9
 

time: 98.2 us -> 99.5 us (1.013)
  the two profiles are of different devices: /device:TPU:24 before, /device:TPU:193 now
where the time goes in v11:
time: 99.5 us; the launch traced here: 99.4 us
  Pallas kernels  97.7 us (98%)
  local copies, waits for them, and re-layouts  1.69 us (2%)
    pallas_call x1, Pallas kernels, on_device(): pl.pallas_call(whole, out_shape=jax.ShapeDtypeStruct((rows, width), low),...  97.7 us

profile of v11, /device:TPU:193, one launch (start us, length us, event | category | flops | bytes accessed | tf_op | source)
XLA Modules:
  0.0 99.4 jit_solution(3954844386968612606)
XLA Ops:
  0.0 97.7 %shard_map.64 = bf16[32,4608]{1,0:T(8,128)(2,1)} custom-call(bf16[32,4608]{1,0:T(8,128)(2,1)} %tokens_ref.1, f32[36,128]{1,0:T(8,128)} %bitcast.3, bf16[4,128,256]{2,1,0:T(8,128)(2,1)} %bitcast.2, bf16[4608,256]{1,0:T(8,128)(2,1)} %wq_ref.1, bf16[4608,128]{1,0:T(8,128)(2,1)} %wk_ref.1, bf16[4608,128]{1,0:T(8,128)(2,1)} %wv_ref.1), custom_call_target="tpu_custom_call" | custom-call | tf_op jit(solution)/shard_map/pallas_call | solution.py:741
  97.7 1.7 %copy.8 = bf16[32,4608]{1,0:T(8,128)(2,1)} copy(bf16[32,4608]{1,0:T(8,128)(2,1)} %shard_map.64) | data formatting | bytes 589824
